TPU v7x, 256 devices: a whole 4x4x8 slice. The times are simulated.
256 devices in a mesh: row: 16 (over z, core), col: 16 (over x, y).
Axes of the slice: x: 4, y: 4, z: 8, core: 2. Of those that a mesh axis runs over, the one named last changes fastest.
Arguments:
- running_cost: float32 [4096, 8192], P('row', 'col'), may hold values from 0.5 to 7.5, as said below
- control_x: float32 [4096, 8192], P('row', 'col'), may hold values from -6 to 6
- control_y: float32 [4096, 8192], P('row', 'col'), may hold values from -6 to 6
- prior_density: float32 [4096, 8192], P('row', 'col'), may hold values from 0.5 to 2
Outputs:
- value_field: float32 [4096, 8192], P('row', 'col')
- density: float32 [4096, 8192], P('row', 'col')
- ergodic: float32 [], replicated
Inputs may be any that keep to these rules, and one draw needn't show every extreme that they name: `running_cost`: strictly positive.
All inputs are finite; a program needn't handle non-finite values.
Results may differ from a plain program's by a relative error of at most 0.0003.
Values sent between devices are 32-bit elements; how exact they have to be, the bound alone decides.
A program may use at most 64 MiB of HBM per device.

v0:
```python
import jax
import jax.numpy as jnp
from jax import lax
from jax.sharding import Mesh
from jax.sharding import PartitionSpec as P

ITERS = 3
ROW = ("row_0", "row_1")
COL = ("col_0", "col_1")


discount_rate = 0.05
diffusion = 0.25


def padded_2(shard, sides, width):
    edges = {}
    for axis, dim in sides:
        count, length = (lax.axis_size(axis), shard.shape[dim])
        up = [(i, (i + 1) % count) for i in range(count - 1)]
        last = lax.slice_in_dim(shard, length - width, length, axis=dim)
        initial = lax.slice_in_dim(shard, 0, width, axis=dim)
        edges[dim] = (
            lax.ppermute(last, axis, up),
            lax.ppermute(initial, axis, [(b, a) for a, b in up]),
        )
    done = []
    for _, dim in sides:
        low, high = edges[dim]
        around = [(width, width) if d in done else (0, 0) for d in range(shard.ndim)]
        shard = jnp.concatenate([jnp.pad(low, around), shard, jnp.pad(high, around)], axis=dim)
        done.append(dim)
    return shard


def from_everyone(shard, axis):
    count = lax.axis_size(axis)
    return lax.all_to_all(
        jnp.broadcast_to(shard[None], (count, *shard.shape)), axis, 0, 0, tiled=True
    )


def of_everyone(shard, axis):
    return from_everyone(shard, axis).sum(axis=0)


def by_axis(shard, axes):
    far, near = axes
    nearer = of_everyone(shard, near)
    return of_everyone(nearer, far)


def together(arrays, axis):
    ends = [0]
    for a in arrays:
        ends.append(ends[-1] + a.size)
    total = by_axis(jnp.concatenate([a.ravel() for a in arrays]), axis)
    return tuple((total[b:e].reshape(a.shape) for a, b, e in zip(arrays, ends, ends[1:])))


def interior(padded):
    return padded[1:-1, 1:-1]


def neighbours(padded):
    return (padded[2:, 1:-1], padded[:-2, 1:-1], padded[1:-1, 2:], padded[1:-1, :-2])


def coefficients(conduct, padded_conduct, zeroth):
    weights = tuple(
        (diffusion * 0.5 * (conduct + outside) for outside in neighbours(padded_conduct))
    )
    center = zeroth + (weights[0] + weights[1] + (weights[2] + weights[3]))
    return (center,) + weights


def operator_apply(padded, coeffs):
    beside = neighbours(padded)
    inflow = (
        coeffs[1] * beside[0]
        + coeffs[2] * beside[1]
        + (coeffs[3] * beside[2] + coeffs[4] * beside[3])
    )
    return coeffs[0] * interior(padded) - inflow


def operate(source, coeffs):
    padded = padded_2(source, ((ROW, 0), (COL, 1)), 1)
    return (padded, operator_apply(padded, coeffs))


def products(residual, applied):
    return together(
        (jnp.sum(residual * residual), jnp.sum(residual * applied)),
        (("row_0", "row_1", "col_0"), "col_1"),
    )


def conjugate(coeffs, forcing, keep_rim):
    solution = jnp.zeros_like(forcing)
    padded_solution = jnp.zeros((forcing.shape[0] + 2, forcing.shape[1] + 2), jnp.float32)
    residual = forcing
    padded_res, applied = operate(residual, coeffs)
    norm_now, product = products(residual, applied)
    step_size = norm_now / product
    direction, image_dir, padded_dir = (residual, applied, padded_res)
    for iteration in range(ITERS):
        solution = solution + step_size * direction
        if keep_rim:
            padded_solution = padded_solution + step_size * padded_dir
        if iteration + 1 < ITERS:
            residual = residual - step_size * image_dir
            padded_res, applied = operate(residual, coeffs)
            norm_next, product = products(residual, applied)
            beta_ratio = norm_next / norm_now
            step_size = norm_next / (product - beta_ratio * norm_next / step_size)
            direction = residual + beta_ratio * direction
            image_dir = applied + beta_ratio * image_dir
            if keep_rim:
                padded_dir = padded_res + beta_ratio * padded_dir
            norm_now = norm_next
    return (solution, padded_solution)


def body(running_cost, control_x, control_y, prior_density):
    control_cost = 0.5 * (control_x * control_x + control_y * control_y)
    conduct = 1.0 + control_cost
    forcing = running_cost + control_cost
    padded_conduct = padded_2(conduct, ((ROW, 0), (COL, 1)), 1)
    bellman = coefficients(conduct, padded_conduct, discount_rate)
    value_field, padded_solution = conjugate(bellman, forcing, True)
    beside = neighbours(padded_solution)
    slope_row = 0.5 * (beside[0] - beside[1])
    slope_col = 0.5 * (beside[2] - beside[3])
    congestion = (slope_row * slope_row + slope_col * slope_col) / (2.0 * diffusion)
    planck = coefficients(conduct, padded_conduct, discount_rate + congestion)
    weighted = jnp.sum(prior_density * (forcing - discount_rate * value_field))
    weight_total = jnp.sum(prior_density)
    density, unused = conjugate(planck, prior_density, False)
    totals = together((weighted, weight_total), (("row_0", "row_1", "col_0"), "col_1"))
    ergodic = totals[0] / totals[1]
    return (value_field, density, ergodic)


def solution(mesh):
    split = Mesh(mesh.devices.reshape(8, 2, 4, 4), ("row_0", "row_1", "col_0", "col_1"))
    return jax.shard_map(
        body,
        mesh=split,
        in_specs=(P(ROW, COL), P(ROW, COL), P(ROW, COL), P(ROW, COL)),
        out_specs=(P(ROW, COL), P(ROW, COL), P()),
        check_vma=False,
    )
```

profile of v0, /device:TPU:1, one launch (start us, length us, event | category | flops | bytes accessed | tf_op | source)
XLA Modules:
  0.0 334.0 jit_solution(6455105443324793532)
XLA Ops:
  0.6 1.5 broadcast_add_fusion
  2.2 4.9 %collective-permute-start.1 = (f32[1,512]{1,0:T(1,128)S(1)}, f32[1,512]{1,0:T(1,128)S(1)}, u32[]{:S(2)}, u32[]{:S(2)}) collective-permute-start(f32[1,512]{1,0:T(1,128)S(1)} %get-tuple-element.49), channel_id=1, source_target_pairs={{0,16},{16,32},{32,48},{48,64},{64,80},{80,96},{96,112},{112,128},... | collective-permute-start | bytes 6152 | tf_op jit(solution)/shard_map/ppermute | solution.py:24
  7.1 1.9 collective-permute-start
  9.2 1.3 collective-permute-start.6
  10.5 4.0 %collective-permute-start.7 = (f32[256,1]{1,0:T(8,128)S(1)}, f32[256,1]{1,0:T(8,128)S(1)}, u32[]{:S(2)}, u32[]{:S(2)}) collective-permute-start(f32[256,1]{1,0:T(8,128)S(1)} %get-tuple-element.42), channel_id=1, source_target_pairs={{0,1},{1,2},{2,3},{3,4},{4,5},{5,6},{6,7},{7,8},{8,9},{9,10},{10,1... | collective-permute-start | bytes 3080 | tf_op jit(solution)/shard_map/ppermute | solution.py:24
  14.6 1.3 collective-permute-start.2
  15.9 4.5 %collective-permute-start.5 = (f32[1,512]{1,0:T(1,128)S(1)}, f32[1,512]{1,0:T(1,128)S(1)}, u32[]{:S(2)}, u32[]{:S(2)}) collective-permute-start(f32[1,512]{1,0:T(1,128)S(1)} %get-tuple-element.43), channel_id=1, source_target_pairs={{0,16},{16,32},{32,48},{48,64},{64,80},{80,96},{96,112},{112,128},... | collective-permute-start | bytes 6152 | tf_op jit(solution)/shard_map/ppermute | solution.py:24
  20.4 1.9 collective-permute-start.4
  22.3 4.0 %collective-permute-start.3 = (f32[256,1]{1,0:T(8,128)S(1)}, f32[256,1]{1,0:T(8,128)S(1)}, u32[]{:S(2)}, u32[]{:S(2)}) collective-permute-start(f32[256,1]{1,0:T(8,128)S(1)} %get-tuple-element.46), channel_id=1, source_target_pairs={{0,1},{1,2},{2,3},{3,4},{4,5},{5,6},{6,7},{7,8},{8,9},{9,10},{10,1... | collective-permute-start | bytes 3080 | tf_op jit(solution)/shard_map/ppermute | solution.py:24
  26.4 1.9 collective-permute-done.3
  28.3 1.4 multiply_reduce_fusion.10
  29.7 1.4 pad_maximum_fusion.49
  31.0 12.1 %all_to_all.84 = f32[4,1,2]{2,1,0:T(1,128)S(1)} all-to-all(f32[4,1,2]{2,1,0:T(1,128)S(1)} %broadcast_in_dim.28), channel_id=1, replica_groups=mesh['row_0'=8,'row_1'=2,'col_0'=4,'col_1'=4] {'col_1'}, dimensions={0} | all-to-all | bytes 64 | tf_op jit(solution)/shard_map/all_to_all | solution.py:38
  43.2 27.1 %all_to_all.85 = f32[64,1,2]{2,1,0:T(1,128)S(1)} all-to-all(f32[64,1,2]{2,1,0:T(1,128)S(1)} %broadcast_in_dim.29), channel_id=1, replica_groups=mesh['row_0'=8,'row_1'=2,'col_0'=4,'col_1'=4] {'row_0','row_1','col_0'}, dimensions={0} | all-to-all | bytes 1024 | tf_op jit(solution)/shard_map/all_to_all | solution.py:38
  72.4 3.1 collective-permute-start.9
  75.5 1.9 collective-permute-start.8
  77.5 1.3 collective-permute-start.10
  78.8 4.0 %collective-permute-start.11 = (f32[256,1]{1,0:T(8,128)S(1)}, f32[256,1]{1,0:T(8,128)S(1)}, u32[]{:S(2)}, u32[]{:S(2)}) collective-permute-start(f32[256,1]{1,0:T(8,128)S(1)} %get-tuple-element.38), channel_id=1, source_target_pairs={{0,1},{1,2},{2,3},{3,4},{4,5},{5,6},{6,7},{7,8},{8,9},{9,10},{10,1... | collective-permute-start | bytes 3080 | tf_op jit(solution)/shard_map/ppermute | solution.py:24
  83.8 1.7 collective-permute-done.11
  85.6 1.5 multiply_reduce_fusion.8
  87.1 1.4 pad_maximum_fusion.50
  88.5 8.2 %all_to_all.86 = f32[4,1,2]{2,1,0:T(1,128)S(1)} all-to-all(f32[4,1,2]{2,1,0:T(1,128)S(1)} %broadcast_in_dim.30), channel_id=1, replica_groups=mesh['row_0'=8,'row_1'=2,'col_0'=4,'col_1'=4] {'col_1'}, dimensions={0} | all-to-all | bytes 64 | tf_op jit(solution)/shard_map/all_to_all | solution.py:38
  96.7 19.0 %all_to_all.87 = f32[64,1,2]{2,1,0:T(1,128)S(1)} all-to-all(f32[64,1,2]{2,1,0:T(1,128)S(1)} %broadcast_in_dim.31), channel_id=1, replica_groups=mesh['row_0'=8,'row_1'=2,'col_0'=4,'col_1'=4] {'row_0','row_1','col_0'}, dimensions={0} | all-to-all | bytes 1024 | tf_op jit(solution)/shard_map/all_to_all | solution.py:38
  121.7 3.2 collective-permute-start.13
  124.9 1.9 collective-permute-start.12
  126.8 2.2 collective-permute-start.15
  129.1 1.3 collective-permute-start.14
  130.4 3.9 %collective-permute-start.17 = (f32[1,512]{1,0:T(1,128)S(1)}, f32[1,512]{1,0:T(1,128)S(1)}, u32[]{:S(2)}, u32[]{:S(2)}) collective-permute-start(f32[1,512]{1,0:T(1,128)S(1)} %get-tuple-element.51), channel_id=1, source_target_pairs={{0,16},{16,32},{32,48},{48,64},{64,80},{80,96},{96,112},{112,128},... | collective-permute-start | bytes 6152 | tf_op jit(solution)/shard_map/ppermute | solution.py:24
  134.3 1.9 collective-permute-start.16
  136.3 1.5 fusion.47
  137.8 1.4 pad_maximum_fusion.51
  139.2 9.0 %all_to_all.88 = f32[4,1,2]{2,1,0:T(1,128)S(1)} all-to-all(f32[4,1,2]{2,1,0:T(1,128)S(1)} %broadcast_in_dim.32), channel_id=1, replica_groups=mesh['row_0'=8,'row_1'=2,'col_0'=4,'col_1'=4] {'col_1'}, dimensions={0} | all-to-all | bytes 64 | tf_op jit(solution)/shard_map/all_to_all | solution.py:38
  148.9 9.8 %all-to-all-start.5 = ((f32[64,1,2]{2,1,0:T(1,128)}), f32[64,1,2]{2,1,0:T(1,128)S(1)}, u32[]{:S(2)}, u32[]{:S(2)}) async-start(f32[64,1,2]{2,1,0:T(1,128)} %broadcast_in_dim.33), calls=%async_computation.5 | async-start | bytes 65536 | tf_op jit(solution)/shard_map/all_to_all | solution.py:38
  160.8 4.6 %collective-permute-start.19 = (f32[256,1]{1,0:T(8,128)}, f32[256,1]{1,0:T(8,128)}, u32[]{:S(2)}, u32[]{:S(2)}) collective-permute-start(f32[256,1]{1,0:T(8,128)} %get-tuple-element.48), channel_id=1, source_target_pairs={{0,1},{1,2},{2,3},{3,4},{4,5},{5,6},{6,7},{7,8},{8,9},{9,10},{10,1... | collective-permute-start | bytes 3080 | tf_op jit(solution)/shard_map/ppermute | solution.py:24
  165.4 2.5 all-to-all-done.5
  172.3 1.8 fusion.1
  174.7 4.7 %multiply_reduce_fusion = (f32[]{:T(128)}, f32[]{:T(128)}, f32[]{:T(128)}, f32[]{:T(128)}, f32[256,512]{1,0:T(8,128)}, /*index=5*/f32[256,512]{1,0:T(8,128)S(1)}, f32[256,512]{1,0:T(8,128)}) fusion(f32[256,512]{1,0:T(8,128)S(1)} %copy-done, f32[256,512]{1,0:T(8,128)S(1)} %get-tuple-element.24, f32[1,512]{1,0:T(1,128)} %collective-permute-done.16, ...), kind=kLoop, calls=%fused_computation.141 | loop fusion | flops 9437180 | bytes 6303780 | tf_op jit(solution)/shard_map/reduce_sum | solution.py:137
  180.7 6.5 %all_to_all.89 = f32[4,1,2]{2,1,0:T(1,128)S(1)} all-to-all(f32[4,1,2]{2,1,0:T(1,128)S(1)} %broadcast_in_dim.34), channel_id=1, replica_groups=mesh['row_0'=8,'row_1'=2,'col_0'=4,'col_1'=4] {'col_1'}, dimensions={0} | all-to-all | bytes 64 | tf_op jit(solution)/shard_map/all_to_all | solution.py:38
  187.2 19.9 %all_to_all.90 = f32[64,1,2]{2,1,0:T(1,128)S(1)} all-to-all(f32[64,1,2]{2,1,0:T(1,128)S(1)} %broadcast_in_dim.35), channel_id=1, replica_groups=mesh['row_0'=8,'row_1'=2,'col_0'=4,'col_1'=4] {'row_0','row_1','col_0'}, dimensions={0} | all-to-all | bytes 1024 | tf_op jit(solution)/shard_map/all_to_all | solution.py:38
  210.3 3.1 collective-permute-start.21
  213.4 1.9 collective-permute-start.20
  215.3 1.3 collective-permute-start.22
  216.6 4.0 %collective-permute-start.23 = (f32[256,1]{1,0:T(8,128)S(1)}, f32[256,1]{1,0:T(8,128)S(1)}, u32[]{:S(2)}, u32[]{:S(2)}) collective-permute-start(f32[256,1]{1,0:T(8,128)S(1)} %get-tuple-element.30), channel_id=1, source_target_pairs={{0,1},{1,2},{2,3},{3,4},{4,5},{5,6},{6,7},{7,8},{8,9},{9,10},{10,1... | collective-permute-start | bytes 3080 | tf_op jit(solution)/shard_map/ppermute | solution.py:24
  220.6 1.4 pad_maximum_fusion.55
  222.0 1.4 collective-permute-done.23
  223.4 2.2 multiply_reduce_fusion.3
  225.6 1.4 pad_maximum_fusion.53
  227.0 8.2 %all_to_all.91 = f32[4,1,2]{2,1,0:T(1,128)S(1)} all-to-all(f32[4,1,2]{2,1,0:T(1,128)S(1)} %broadcast_in_dim.36), channel_id=1, replica_groups=mesh['row_0'=8,'row_1'=2,'col_0'=4,'col_1'=4] {'col_1'}, dimensions={0} | all-to-all | bytes 64 | tf_op jit(solution)/shard_map/all_to_all | solution.py:38
  235.8 3.2 all-to-all-start.12
  239.1 4.1 %all-to-all-done.12 = f32[4,1,2]{2,1,0:T(1,128)S(1)} async-done(((f32[4,1,2]{2,1,0:T(1,128)}), f32[4,1,2]{2,1,0:T(1,128)S(1)}, u32[]{:S(2)}, u32[]{:S(2)}) %all-to-all-start.12) | async-done | bytes 64 | tf_op jit(solution)/shard_map/all_to_all | solution.py:38
  243.8 11.1 %all-to-all-start.9 = ((f32[64,1,2]{2,1,0:T(1,128)}), f32[64,1,2]{2,1,0:T(1,128)S(1)}, u32[]{:S(2)}, u32[]{:S(2)}) async-start(f32[64,1,2]{2,1,0:T(1,128)} %broadcast_in_dim.37), calls=%async_computation.9 | async-start | bytes 65536 | tf_op jit(solution)/shard_map/all_to_all | solution.py:38
  254.9 9.2 %all-to-all-done.9 = f32[64,1,2]{2,1,0:T(1,128)S(1)} async-done(((f32[64,1,2]{2,1,0:T(1,128)}), f32[64,1,2]{2,1,0:T(1,128)S(1)}, u32[]{:S(2)}, u32[]{:S(2)}) %all-to-all-start.9) | async-done | bytes 544 | tf_op jit(solution)/shard_map/all_to_all | solution.py:38
  264.7 5.8 %all-to-all-start.13 = ((f32[64,1,2]{2,1,0:T(1,128)}), f32[64,1,2]{2,1,0:T(1,128)}, u32[]{:S(2)}, u32[]{:S(2)}) async-start(f32[64,1,2]{2,1,0:T(1,128)} %broadcast_in_dim.41), calls=%async_computation.13 | async-start | bytes 65536 | tf_op jit(solution)/shard_map/all_to_all | solution.py:38
  275.8 1.8 multiply_reduce_fusion.1
  277.6 3.6 %collective-permute-start.25 = (f32[1,512]{1,0:T(1,128)S(1)}, f32[1,512]{1,0:T(1,128)S(1)}, u32[]{:S(2)}, u32[]{:S(2)}) collective-permute-start(f32[1,512]{1,0:T(1,128)S(1)} %get-tuple-element.27), channel_id=1, source_target_pairs={{0,16},{16,32},{32,48},{48,64},{64,80},{80,96},{96,112},{112,128},... | collective-permute-start | bytes 6152 | tf_op jit(solution)/shard_map/ppermute | solution.py:24
  281.2 1.9 collective-permute-start.24
  283.2 1.3 collective-permute-start.26
  284.5 4.0 %collective-permute-start.27 = (f32[256,1]{1,0:T(8,128)S(1)}, f32[256,1]{1,0:T(8,128)S(1)}, u32[]{:S(2)}, u32[]{:S(2)}) collective-permute-start(f32[256,1]{1,0:T(8,128)S(1)} %get-tuple-element.26), channel_id=1, source_target_pairs={{0,1},{1,2},{2,3},{3,4},{4,5},{5,6},{6,7},{7,8},{8,9},{9,10},{10,1... | collective-permute-start | bytes 3080 | tf_op jit(solution)/shard_map/ppermute | solution.py:24
  289.4 1.4 collective-permute-done.27
  290.8 1.4 fusion.8
  292.1 1.4 pad_maximum_fusion.54
  293.5 8.2 %all_to_all.92 = f32[4,1,2]{2,1,0:T(1,128)S(1)} all-to-all(f32[4,1,2]{2,1,0:T(1,128)S(1)} %broadcast_in_dim.38), channel_id=1, replica_groups=mesh['row_0'=8,'row_1'=2,'col_0'=4,'col_1'=4] {'col_1'}, dimensions={0} | all-to-all | bytes 64 | tf_op jit(solution)/shard_map/all_to_all | solution.py:38
  302.4 15.6 %all-to-all-start.11 = ((f32[64,1,2]{2,1,0:T(1,128)}), f32[64,1,2]{2,1,0:T(1,128)S(1)}, u32[]{:S(2)}, u32[]{:S(2)}) async-start(f32[64,1,2]{2,1,0:T(1,128)} %broadcast_in_dim.39), calls=%async_computation.11 | async-start | bytes 65536 | tf_op jit(solution)/shard_map/all_to_all | solution.py:38
  319.9 7.1 %all-to-all-done.11 = f32[64,1,2]{2,1,0:T(1,128)S(1)} async-done(((f32[64,1,2]{2,1,0:T(1,128)}), f32[64,1,2]{2,1,0:T(1,128)S(1)}, u32[]{:S(2)}, u32[]{:S(2)}) %all-to-all-start.11) | async-done | bytes 544 | tf_op jit(solution)/shard_map/all_to_all | solution.py:38
  (112 shorter events, 17.6 us)
Async XLA Ops:
  2.2 26.1 %collective-permute-start.1 = (f32[1,512]{1,0:T(1,128)S(1)}, f32[1,512]{1,0:T(1,128)S(1)}, u32[]{:S(2)}, u32[]{:S(2)}) collective-permute-start(f32[1,512]{1,0:T(1,128)S(1)} %get-tuple-element.49), channel_id=1, source_target_pairs={{0,16},{16,32},{32,48},{48,64},{64,80},{80,96},{96,112},{112,128},... | collective-permute-start | bytes 6152 | tf_op jit(solution)/shard_map/ppermute | solution.py:24
  7.1 21.1 %collective-permute-start = (f32[1,512]{1,0:T(1,128)S(1)}, f32[1,512]{1,0:T(1,128)S(1)}, u32[]{:S(2)}, u32[]{:S(2)}) collective-permute-start(f32[1,512]{1,0:T(1,128)S(1)} %get-tuple-element.50), channel_id=1, source_target_pairs={{16,0},{32,16},{48,32},{64,48},{80,64},{96,80},{112,96},{128,112},... | collective-permute-start | bytes 6152 | tf_op jit(solution)/shard_map/ppermute | solution.py:25
  9.2 6.7 %collective-permute-start.6 = (f32[256,1]{1,0:T(8,128)S(1)}, f32[256,1]{1,0:T(8,128)S(1)}, u32[]{:S(2)}, u32[]{:S(2)}) collective-permute-start(f32[256,1]{1,0:T(8,128)S(1)} %get-tuple-element.41), channel_id=1, source_target_pairs={{1,0},{2,1},{3,2},{4,3},{5,4},{6,5},{7,6},{8,7},{9,8},{10,9},{11,1... | collective-permute-start | bytes 3080 | tf_op jit(solution)/shard_map/ppermute | solution.py:25
  10.5 9.9 %collective-permute-start.7 = (f32[256,1]{1,0:T(8,128)S(1)}, f32[256,1]{1,0:T(8,128)S(1)}, u32[]{:S(2)}, u32[]{:S(2)}) collective-permute-start(f32[256,1]{1,0:T(8,128)S(1)} %get-tuple-element.42), channel_id=1, source_target_pairs={{0,1},{1,2},{2,3},{3,4},{4,5},{5,6},{6,7},{7,8},{8,9},{9,10},{10,1... | collective-permute-start | bytes 3080 | tf_op jit(solution)/shard_map/ppermute | solution.py:24
  14.6 7.8 %collective-permute-start.2 = (f32[256,1]{1,0:T(8,128)S(1)}, f32[256,1]{1,0:T(8,128)S(1)}, u32[]{:S(2)}, u32[]{:S(2)}) collective-permute-start(f32[256,1]{1,0:T(8,128)S(1)} %get-tuple-element.45), channel_id=1, source_target_pairs={{1,0},{2,1},{3,2},{4,3},{5,4},{6,5},{7,6},{8,7},{9,8},{10,9},{11,1... | collective-permute-start | bytes 3080 | tf_op jit(solution)/shard_map/ppermute | solution.py:25
  15.9 12.4 %collective-permute-start.5 = (f32[1,512]{1,0:T(1,128)S(1)}, f32[1,512]{1,0:T(1,128)S(1)}, u32[]{:S(2)}, u32[]{:S(2)}) collective-permute-start(f32[1,512]{1,0:T(1,128)S(1)} %get-tuple-element.43), channel_id=1, source_target_pairs={{0,16},{16,32},{32,48},{48,64},{64,80},{80,96},{96,112},{112,128},... | collective-permute-start | bytes 6152 | tf_op jit(solution)/shard_map/ppermute | solution.py:24
  20.4 7.9 %collective-permute-start.4 = (f32[1,512]{1,0:T(1,128)S(1)}, f32[1,512]{1,0:T(1,128)S(1)}, u32[]{:S(2)}, u32[]{:S(2)}) collective-permute-start(f32[1,512]{1,0:T(1,128)S(1)} %get-tuple-element.44), channel_id=1, source_target_pairs={{16,0},{32,16},{48,32},{64,48},{80,64},{96,80},{112,96},{128,112},... | collective-permute-start | bytes 6152 | tf_op jit(solution)/shard_map/ppermute | solution.py:25
  22.3 5.9 %collective-permute-start.3 = (f32[256,1]{1,0:T(8,128)S(1)}, f32[256,1]{1,0:T(8,128)S(1)}, u32[]{:S(2)}, u32[]{:S(2)}) collective-permute-start(f32[256,1]{1,0:T(8,128)S(1)} %get-tuple-element.46), channel_id=1, source_target_pairs={{0,1},{1,2},{2,3},{3,4},{4,5},{5,6},{6,7},{7,8},{8,9},{9,10},{10,1... | collective-permute-start | bytes 3080 | tf_op jit(solution)/shard_map/ppermute | solution.py:24
  26.4 3.3 copy-start.2
  28.3 1.4 copy-start.6
  72.4 13.2 %collective-permute-start.9 = (f32[1,512]{1,0:T(1,128)S(1)}, f32[1,512]{1,0:T(1,128)S(1)}, u32[]{:S(2)}, u32[]{:S(2)}) collective-permute-start(f32[1,512]{1,0:T(1,128)S(1)} %get-tuple-element.39), channel_id=1, source_target_pairs={{0,16},{16,32},{32,48},{48,64},{64,80},{80,96},{96,112},{112,128},... | collective-permute-start | bytes 6152 | tf_op jit(solution)/shard_map/ppermute | solution.py:24
  75.5 10.1 %collective-permute-start.8 = (f32[1,512]{1,0:T(1,128)S(1)}, f32[1,512]{1,0:T(1,128)S(1)}, u32[]{:S(2)}, u32[]{:S(2)}) collective-permute-start(f32[1,512]{1,0:T(1,128)S(1)} %get-tuple-element.40), channel_id=1, source_target_pairs={{16,0},{32,16},{48,32},{64,48},{80,64},{96,80},{112,96},{128,112},... | collective-permute-start | bytes 6152 | tf_op jit(solution)/shard_map/ppermute | solution.py:25
  77.5 6.3 %collective-permute-start.10 = (f32[256,1]{1,0:T(8,128)S(1)}, f32[256,1]{1,0:T(8,128)S(1)}, u32[]{:S(2)}, u32[]{:S(2)}) collective-permute-start(f32[256,1]{1,0:T(8,128)S(1)} %get-tuple-element.37), channel_id=1, source_target_pairs={{1,0},{2,1},{3,2},{4,3},{5,4},{6,5},{7,6},{8,7},{9,8},{10,9},{11,1... | collective-permute-start | bytes 3080 | tf_op jit(solution)/shard_map/ppermute | solution.py:25
  78.8 6.8 %collective-permute-start.11 = (f32[256,1]{1,0:T(8,128)S(1)}, f32[256,1]{1,0:T(8,128)S(1)}, u32[]{:S(2)}, u32[]{:S(2)}) collective-permute-start(f32[256,1]{1,0:T(8,128)S(1)} %get-tuple-element.38), channel_id=1, source_target_pairs={{0,1},{1,2},{2,3},{3,4},{4,5},{5,6},{6,7},{7,8},{8,9},{9,10},{10,1... | collective-permute-start | bytes 3080 | tf_op jit(solution)/shard_map/ppermute | solution.py:24
  83.8 3.3 copy-start.4
  85.6 1.5 copy-start.5
  85.6 1.5 copy-start.8
  85.6 1.5 copy-start.10
  121.6 8.7 %copy-start = (f32[256,512]{1,0:T(8,128)S(1)}, f32[256,512]{1,0:T(8,128)}, u32[]{:S(2)}) copy-start(f32[256,512]{1,0:T(8,128)} %param.7) | copy-start | bytes 1572868
  121.7 14.6 %collective-permute-start.13 = (f32[1,512]{1,0:T(1,128)S(1)}, f32[1,512]{1,0:T(1,128)S(1)}, u32[]{:S(2)}, u32[]{:S(2)}) collective-permute-start(f32[1,512]{1,0:T(1,128)S(1)} %get-tuple-element.35), channel_id=1, source_target_pairs={{0,16},{16,32},{32,48},{48,64},{64,80},{80,96},{96,112},{112,128},... | collective-permute-start | bytes 6152 | tf_op jit(solution)/shard_map/ppermute | solution.py:24
  124.9 11.4 %collective-permute-start.12 = (f32[1,512]{1,0:T(1,128)S(1)}, f32[1,512]{1,0:T(1,128)S(1)}, u32[]{:S(2)}, u32[]{:S(2)}) collective-permute-start(f32[1,512]{1,0:T(1,128)S(1)} %get-tuple-element.36), channel_id=1, source_target_pairs={{16,0},{32,16},{48,32},{64,48},{80,64},{96,80},{112,96},{128,112},... | collective-permute-start | bytes 6152 | tf_op jit(solution)/shard_map/ppermute | solution.py:25
  126.8 7.5 %collective-permute-start.15 = (f32[256,1]{1,0:T(8,128)S(1)}, f32[256,1]{1,0:T(8,128)S(1)}, u32[]{:S(2)}, u32[]{:S(2)}) collective-permute-start(f32[256,1]{1,0:T(8,128)S(1)} %get-tuple-element.33), channel_id=1, source_target_pairs={{0,1},{1,2},{2,3},{3,4},{4,5},{5,6},{6,7},{7,8},{8,9},{9,10},{10,1... | collective-permute-start | bytes 3080 | tf_op jit(solution)/shard_map/ppermute | solution.py:24
  129.1 7.2 %collective-permute-start.14 = (f32[256,1]{1,0:T(8,128)S(1)}, f32[256,1]{1,0:T(8,128)S(1)}, u32[]{:S(2)}, u32[]{:S(2)}) collective-permute-start(f32[256,1]{1,0:T(8,128)S(1)} %get-tuple-element.34), channel_id=1, source_target_pairs={{1,0},{2,1},{3,2},{4,3},{5,4},{6,5},{7,6},{8,7},{9,8},{10,9},{11,1... | collective-permute-start | bytes 3080 | tf_op jit(solution)/shard_map/ppermute | solution.py:25
  130.4 43.7 %collective-permute-start.17 = (f32[1,512]{1,0:T(1,128)S(1)}, f32[1,512]{1,0:T(1,128)S(1)}, u32[]{:S(2)}, u32[]{:S(2)}) collective-permute-start(f32[1,512]{1,0:T(1,128)S(1)} %get-tuple-element.51), channel_id=1, source_target_pairs={{0,16},{16,32},{32,48},{48,64},{64,80},{80,96},{96,112},{112,128},... | collective-permute-start | bytes 6152 | tf_op jit(solution)/shard_map/ppermute | solution.py:24
  134.3 40.4 %collective-permute-start.16 = (f32[1,512]{1,0:T(1,128)S(1)}, f32[1,512]{1,0:T(1,128)}, u32[]{:S(2)}, u32[]{:S(2)}) collective-permute-start(f32[1,512]{1,0:T(1,128)S(1)} %get-tuple-element.52), channel_id=1, source_target_pairs={{16,0},{32,16},{48,32},{64,48},{80,64},{96,80},{112,96},{128,112},... | collective-permute-start | bytes 6152 | tf_op jit(solution)/shard_map/ppermute | solution.py:25
  148.9 19.0 %all-to-all-start.5 = ((f32[64,1,2]{2,1,0:T(1,128)}), f32[64,1,2]{2,1,0:T(1,128)S(1)}, u32[]{:S(2)}, u32[]{:S(2)}) async-start(f32[64,1,2]{2,1,0:T(1,128)} %broadcast_in_dim.33), calls=%async_computation.5 | async-start | bytes 65536 | tf_op jit(solution)/shard_map/all_to_all | solution.py:38
  158.7 13.6 %copy-start.3 = (f32[258,1]{1,0:T(8,128)S(1)}, f32[258,1]{1,0:T(8,128)}, u32[]{:S(2)}) copy-start(f32[258,1]{1,0:T(8,128)} %copy-done.2) | copy-start | bytes 3100
  158.7 13.6 %copy-start.11 = (f32[1,512]{1,0:T(1,128)S(1)}, f32[1,512]{1,0:T(1,128)}, u32[]{:S(2)}) copy-start(f32[1,512]{1,0:T(1,128)} %copy-done.10) | copy-start | bytes 6148
  159.5 14.6 %collective-permute-start.18 = (f32[256,1]{1,0:T(8,128)}, f32[256,1]{1,0:T(8,128)}, u32[]{:S(2)}, u32[]{:S(2)}) collective-permute-start(f32[256,1]{1,0:T(8,128)} %get-tuple-element.47), channel_id=1, source_target_pairs={{1,0},{2,1},{3,2},{4,3},{5,4},{6,5},{7,6},{8,7},{9,8},{10,9},{11,1... | collective-permute-start | bytes 3080 | tf_op jit(solution)/shard_map/ppermute | solution.py:25
  160.8 13.3 %collective-permute-start.19 = (f32[256,1]{1,0:T(8,128)}, f32[256,1]{1,0:T(8,128)}, u32[]{:S(2)}, u32[]{:S(2)}) collective-permute-start(f32[256,1]{1,0:T(8,128)} %get-tuple-element.48), channel_id=1, source_target_pairs={{0,1},{1,2},{2,3},{3,4},{4,5},{5,6},{6,7},{7,8},{8,9},{9,10},{10,1... | collective-permute-start | bytes 3080 | tf_op jit(solution)/shard_map/ppermute | solution.py:24
  171.0 1.3 copy-start.9
  171.0 1.3 copy-start.7
  174.1 0.6 copy-start.12
  210.3 13.1 %collective-permute-start.21 = (f32[1,512]{1,0:T(1,128)S(1)}, f32[1,512]{1,0:T(1,128)S(1)}, u32[]{:S(2)}, u32[]{:S(2)}) collective-permute-start(f32[1,512]{1,0:T(1,128)S(1)} %get-tuple-element.31), channel_id=1, source_target_pairs={{0,16},{16,32},{32,48},{48,64},{64,80},{80,96},{96,112},{112,128},... | collective-permute-start | bytes 6152 | tf_op jit(solution)/shard_map/ppermute | solution.py:24
  213.4 10.0 %collective-permute-start.20 = (f32[1,512]{1,0:T(1,128)S(1)}, f32[1,512]{1,0:T(1,128)S(1)}, u32[]{:S(2)}, u32[]{:S(2)}) collective-permute-start(f32[1,512]{1,0:T(1,128)S(1)} %get-tuple-element.32), channel_id=1, source_target_pairs={{16,0},{32,16},{48,32},{64,48},{80,64},{96,80},{112,96},{128,112},... | collective-permute-start | bytes 6152 | tf_op jit(solution)/shard_map/ppermute | solution.py:25
  215.3 6.7 %collective-permute-start.22 = (f32[256,1]{1,0:T(8,128)S(1)}, f32[256,1]{1,0:T(8,128)S(1)}, u32[]{:S(2)}, u32[]{:S(2)}) collective-permute-start(f32[256,1]{1,0:T(8,128)S(1)} %get-tuple-element.29), channel_id=1, source_target_pairs={{1,0},{2,1},{3,2},{4,3},{5,4},{6,5},{7,6},{8,7},{9,8},{10,9},{11,1... | collective-permute-start | bytes 3080 | tf_op jit(solution)/shard_map/ppermute | solution.py:25
  216.6 6.8 %collective-permute-start.23 = (f32[256,1]{1,0:T(8,128)S(1)}, f32[256,1]{1,0:T(8,128)S(1)}, u32[]{:S(2)}, u32[]{:S(2)}) collective-permute-start(f32[256,1]{1,0:T(8,128)S(1)} %get-tuple-element.30), channel_id=1, source_target_pairs={{0,1},{1,2},{2,3},{3,4},{4,5},{5,6},{6,7},{7,8},{8,9},{9,10},{10,1... | collective-permute-start | bytes 3080 | tf_op jit(solution)/shard_map/ppermute | solution.py:24
  223.4 52.4 %copy-start.1 = (f32[256,512]{1,0:T(8,128)S(1)}, f32[256,512]{1,0:T(8,128)}, u32[]{:S(2)}) copy-start(f32[256,512]{1,0:T(8,128)} %get-tuple-element.16) | copy-start | bytes 1572868
  235.8 7.4 %all-to-all-start.12 = ((f32[4,1,2]{2,1,0:T(1,128)}), f32[4,1,2]{2,1,0:T(1,128)S(1)}, u32[]{:S(2)}, u32[]{:S(2)}) async-start(f32[4,1,2]{2,1,0:T(1,128)} %broadcast_in_dim.40), calls=%async_computation.12 | async-start | bytes 4096 | tf_op jit(solution)/shard_map/all_to_all | solution.py:38
  243.8 20.3 %all-to-all-start.9 = ((f32[64,1,2]{2,1,0:T(1,128)}), f32[64,1,2]{2,1,0:T(1,128)S(1)}, u32[]{:S(2)}, u32[]{:S(2)}) async-start(f32[64,1,2]{2,1,0:T(1,128)} %broadcast_in_dim.37), calls=%async_computation.9 | async-start | bytes 65536 | tf_op jit(solution)/shard_map/all_to_all | solution.py:38
  264.7 23.9 %all-to-all-start.13 = ((f32[64,1,2]{2,1,0:T(1,128)}), f32[64,1,2]{2,1,0:T(1,128)}, u32[]{:S(2)}, u32[]{:S(2)}) async-start(f32[64,1,2]{2,1,0:T(1,128)} %broadcast_in_dim.41), calls=%async_computation.13 | async-start | bytes 65536 | tf_op jit(solution)/shard_map/all_to_all | solution.py:38
  277.6 13.1 %collective-permute-start.25 = (f32[1,512]{1,0:T(1,128)S(1)}, f32[1,512]{1,0:T(1,128)S(1)}, u32[]{:S(2)}, u32[]{:S(2)}) collective-permute-start(f32[1,512]{1,0:T(1,128)S(1)} %get-tuple-element.27), channel_id=1, source_target_pairs={{0,16},{16,32},{32,48},{48,64},{64,80},{80,96},{96,112},{112,128},... | collective-permute-start | bytes 6152 | tf_op jit(solution)/shard_map/ppermute | solution.py:24
  281.2 9.6 %collective-permute-start.24 = (f32[1,512]{1,0:T(1,128)S(1)}, f32[1,512]{1,0:T(1,128)S(1)}, u32[]{:S(2)}, u32[]{:S(2)}) collective-permute-start(f32[1,512]{1,0:T(1,128)S(1)} %get-tuple-element.28), channel_id=1, source_target_pairs={{16,0},{32,16},{48,32},{64,48},{80,64},{96,80},{112,96},{128,112},... | collective-permute-start | bytes 6152 | tf_op jit(solution)/shard_map/ppermute | solution.py:25
  283.2 6.2 %collective-permute-start.26 = (f32[256,1]{1,0:T(8,128)S(1)}, f32[256,1]{1,0:T(8,128)S(1)}, u32[]{:S(2)}, u32[]{:S(2)}) collective-permute-start(f32[256,1]{1,0:T(8,128)S(1)} %get-tuple-element.25), channel_id=1, source_target_pairs={{1,0},{2,1},{3,2},{4,3},{5,4},{6,5},{7,6},{8,7},{9,8},{10,9},{11,1... | collective-permute-start | bytes 3080 | tf_op jit(solution)/shard_map/ppermute | solution.py:25
  284.5 6.3 %collective-permute-start.27 = (f32[256,1]{1,0:T(8,128)S(1)}, f32[256,1]{1,0:T(8,128)S(1)}, u32[]{:S(2)}, u32[]{:S(2)}) collective-permute-start(f32[256,1]{1,0:T(8,128)S(1)} %get-tuple-element.26), channel_id=1, source_target_pairs={{0,1},{1,2},{2,3},{3,4},{4,5},{5,6},{6,7},{7,8},{8,9},{9,10},{10,1... | collective-permute-start | bytes 3080 | tf_op jit(solution)/shard_map/ppermute | solution.py:24
  302.4 24.7 %all-to-all-start.11 = ((f32[64,1,2]{2,1,0:T(1,128)}), f32[64,1,2]{2,1,0:T(1,128)S(1)}, u32[]{:S(2)}, u32[]{:S(2)}) async-start(f32[64,1,2]{2,1,0:T(1,128)} %broadcast_in_dim.39), calls=%async_computation.11 | async-start | bytes 65536 | tf_op jit(solution)/shard_map/all_to_all | solution.py:38
where the time goes:
time: 336 us; the launch traced here: 334 us
  starting transfers between devices  121 us (36%)
  blocking collectives  118 us (35%)
  other arithmetic  31.9 us (9%)
  waiting for transfers between devices  30.3 us (9%)
  between operations  23.2 us (7%)
  local copies, waits for them, and re-layouts  9.5 us (3%)
    all_to_all x9, blocking collectives, from_everyone(): lax.all_to_all(jnp.broadcast_to(shard[None], (count, *shard.shape)), axis...  118 us
    ppermute x14, starting transfers between devices, padded_2(): lax.ppermute(last, axis, up)  53 us
    all_to_all x5, starting transfers between devices, from_everyone(): lax.all_to_all(jnp.broadcast_to(shard[None], (count, *shard.shape)), axis...  45.5 us
    all_to_all x5, waiting for transfers between devices, from_everyone(): lax.all_to_all(jnp.broadcast_to(shard[None], (count, *shard.shape)), axis...  22.9 us
    ppermute x14, starting transfers between devices, padded_2(): lax.ppermute(initial, axis, [(b, a) for a, b in up])  22.5 us
    concatenate x7, other arithmetic, together(): total = by_axis(jnp.concatenate([a.ravel() for a in arrays]), axis)  9.58 us
    reduce_sum x5, other arithmetic, products(): jnp.sum(residual * residual)  7.68 us
  transfers between devices with their start and end apart: 33, of which 9 were waited for; matrix products, arithmetic and copies ran while one was open for 4% of the time, Pallas kernels for 0%

commit v1 on v0

v1 whole, which is shorter than its diff:
```python
import functools

import jax
import jax.numpy as jnp
from jax import lax
from jax.experimental import pallas as pl
from jax.experimental.pallas import tpu as pltpu
from jax.sharding import PartitionSpec as P

MESH = pl.DeviceIdType.MESH

SCALE = 1.0 / 64.0
FACE = 0.25 * 0.5 * SCALE
DISCOUNT = 0.05

LANE = 128
TOP = 16
HALO = 8
STEP = 16


def solve(nu):
    shift = DISCOUNT * SCALE
    m = [nu[k + 1] + shift * nu[k] for k in range(5)]
    l1 = m[1] / m[0]
    l2 = m[2] / m[0]
    d1 = m[2] - l1 * m[1]
    e = m[3] - l2 * m[1]
    l3 = e / d1
    d2 = (m[4] - l2 * m[2]) - l3 * e
    y0 = nu[0]
    y1 = nu[1] - l1 * y0
    y2 = (nu[2] - l2 * y0) - l3 * y1
    c2 = y2 / d2
    c1 = y1 / d1 - l3 * c2
    c0 = y0 / m[0] - l1 * c1 - l2 * c2
    return c0 * SCALE, c1 * SCALE, c2 * SCALE


def kernel(
    nrow, ncol, rows, tiles,
    rc_hbm, cx_hbm, cy_hbm, pr_hbm,
    val_hbm, den_hbm, erg_ref,
    cx, cy, rc, C, B, Q, WE, WW, WS, CE, V1, V2, X, LP, U1, U2, Y,
    pack_e, pack_w, from_w, from_e, ga, gb, gc, gd,
    in_sem, out_sem, hs_sem, hr_sem, as_sem, ar_sem,
):
    me_r = lax.axis_index("row")
    me_c = lax.axis_index("col")
    up, down = lax.rem(me_r + nrow - 1, nrow), lax.rem(me_r + 1, nrow)
    west, east = lax.rem(me_c + ncol - 1, ncol), lax.rem(me_c + 1, ncol)
    ext = tiles + 1
    END = TOP + rows

    def tile_of(ref, j):
        return ref.at[:, pl.ds(j * LANE, LANE)]

    loads = {}
    for n, (src, dst, top) in enumerate(((cx_hbm, cx, 0), (cy_hbm, cy, 0), (rc_hbm, rc, 0), (pr_hbm, Q, TOP))):
        for j in range(tiles):
            copy = pltpu.make_async_copy(tile_of(src, j), dst.at[j, pl.ds(top, rows), :], in_sem.at[n, j])
            copy.start()
            loads[n, j] = copy

    barrier = pltpu.get_barrier_semaphore()
    met = 0
    for d in range(1, nrow):
        pl.semaphore_signal(barrier, inc=1, device_id=(lax.rem(me_r + d, nrow), me_c), device_id_type=MESH)
        met += 1
    for d in range(1, ncol):
        pl.semaphore_signal(barrier, inc=1, device_id=(me_r, lax.rem(me_c + d, ncol)), device_id_type=MESH)
        met += 1
    for r in (up, down):
        for c in (west, east):
            pl.semaphore_signal(barrier, inc=1, device_id=(r, c), device_id_type=MESH)
            met += 1

    zero = jnp.zeros((8, LANE), jnp.float32)
    for ref in (C, B, Q, WS, V1, V2, X, U1, U2):
        for j in range(ext):
            ref[j, pl.ds(0, 8), :] = zero
            ref[j, pl.ds(END + HALO, 8), :] = zero

    for copy in loads.values():
        copy.wait()

    def first(i, carry):
        r = pl.multiple_of(i * STEP, STEP)
        for j in range(tiles):
            a, b = cx[j, pl.ds(r, STEP), :], cy[j, pl.ds(r, STEP), :]
            cost = 0.5 * (a * a + b * b)
            C[j, pl.ds(TOP + r, STEP), :] = (1.0 + cost) * FACE
            B[j, pl.ds(TOP + r, STEP), :] = rc[j, pl.ds(r, STEP), :] + cost
        return carry

    lax.fori_loop(0, rows // STEP, first, 0)

    parts = LANE // 16
    pile = rows // parts
    lane = lax.broadcasted_iota(jnp.int32, (pile, LANE), 1)
    slot = lane & 15
    is_c, is_b = slot < 6, slot < 11
    acc_e = jnp.zeros((pile, LANE), jnp.float32)
    acc_w = jnp.zeros((pile, LANE), jnp.float32)
    for k in range(parts):
        at = pl.ds(TOP + pile * k, pile)
        here = (lane >> 4) == k
        got = []
        for j, firsts in ((tiles - 1, (122, 123, 125)), (0, (0, 0, 0))):
            rolled = [
                pltpu.roll(f[j, at, :], (16 * k + o - s) % LANE, 1)
                for f, o, s in zip((C, B, Q), (0, 6, 11), firsts)
            ]
            got.append(jnp.where(is_c, rolled[0], jnp.where(is_b, rolled[1], rolled[2])))
        acc_e = jnp.where(here, got[0], acc_e)
        acc_w = jnp.where(here, got[1], acc_w)
    pack_e[...] = acc_e
    pack_w[...] = acc_w

    pl.semaphore_wait(barrier, met)

    sends = []

    def send(src, dst, to):
        n = len(sends)
        copy = pltpu.make_async_remote_copy(
            src_ref=src, dst_ref=dst, send_sem=hs_sem.at[n], recv_sem=hr_sem.at[n],
            device_id=to, device_id_type=MESH,
        )
        copy.start()
        sends.append(copy)

    send(pack_e, from_w.at[pl.ds(0, pile), :], (me_r, east))
    send(pack_w, from_e.at[pl.ds(0, pile), :], (me_r, west))
    low, high = pl.ds(0, 8), pl.ds(pile - 8, 8)
    sw_at, nw_at = pl.ds(pile, 8), pl.ds(pile + 8, 8)
    send(pack_e.at[high, :], from_w.at[nw_at, :], (down, east))
    send(pack_e.at[low, :], from_w.at[sw_at, :], (up, east))
    send(pack_w.at[high, :], from_e.at[nw_at, :], (down, west))
    send(pack_w.at[low, :], from_e.at[sw_at, :], (up, west))
    body = pl.ds(0, tiles)
    for f in (C, B, Q):
        send(f.at[body, pl.ds(TOP, HALO), :], f.at[body, pl.ds(END, HALO), :], (up, me_c))
        send(f.at[body, pl.ds(END - HALO, HALO), :], f.at[body, pl.ds(TOP - HALO, HALO), :], (down, me_c))

    for copy in sends:
        copy.wait_recv()

    one, nil = jnp.float32(1.0), jnp.float32(0.0)
    has_n = jnp.where(me_r > 0, one, nil)
    has_s = jnp.where(me_r < nrow - 1, one, nil)
    has_w = jnp.where(me_c > 0, one, nil)
    has_e = jnp.where(me_c < ncol - 1, one, nil)

    def unpack(at, src, k, n, keep):
        w = from_w[src, :] * (has_w * keep)
        e = from_e[src, :] * (has_e * keep)
        l = lax.broadcasted_iota(jnp.int32, (n, LANE), 1)
        for f, o, s, wide in zip((C, B, Q), (0, 6, 11), (122, 123, 125), (6, 5, 3)):
            rw = pltpu.roll(w, (s - 16 * k - o) % LANE, 1)
            re = pltpu.roll(e, (-16 * k - o) % LANE, 1)
            f[tiles, at, :] = jnp.where(l >= s, rw, jnp.where(l < wide, re, 0.0))

    for k in range(parts):
        unpack(pl.ds(TOP + pile * k, pile), pl.ds(0, pile), k, pile, one)
    unpack(pl.ds(TOP - HALO, HALO), nw_at, parts - 1, HALO, has_n)
    unpack(pl.ds(END, HALO), sw_at, 0, HALO, has_s)

    @pl.when(me_r == 0)
    def _():
        for f in (C, B, Q):
            for j in range(tiles):
                f[j, pl.ds(TOP - HALO, HALO), :] = zero

    @pl.when(me_r == nrow - 1)
    def _():
        for f in (C, B, Q):
            for j in range(tiles):
                f[j, pl.ds(END, HALO), :] = zero

    lane1 = lax.broadcasted_iota(jnp.int32, (1, LANE), 1)
    inside = jnp.where(lane1 < LANE // 2, has_e, has_w)

    def masks(n):
        l = lax.broadcasted_iota(jnp.int32, (n, LANE), 1)
        return l == LANE - 1, l == 0

    def to_east(vs, last):
        r = [pltpu.roll(v, LANE - 1, 1) for v in vs]
        return [jnp.where(last, r[(j + 1) % ext], r[j]) for j in range(ext)]

    def to_west(vs, start):
        r = [pltpu.roll(v, 1, 1) for v in vs]
        return [jnp.where(start, r[(j - 1) % ext], r[j]) for j in range(ext)]

    def rows_of(ref, r, n):
        return [ref[j, pl.ds(r, n), :] for j in range(ext)]

    def keep_in(vs, keep):
        vs = vs[:tiles] + [vs[tiles] * inside]
        return vs if keep is None else [v * keep for v in vs]

    def put(ref, r, n, vs):
        for j, v in enumerate(vs):
            ref[j, pl.ds(r, n), :] = v

    def fold(acc, v):
        for s in range(0, v.shape[0], 8):
            acc = acc + v[s : s + 8, :]
        return acc

    def add(accs, lists):
        out = []
        for acc, (p, q) in zip(accs, lists):
            total = None
            for j in range(tiles):
                t = p[j] if q is None else p[j] * q[j]
                total = t if total is None else total + t
            out.append(fold(acc, total))
        return tuple(out)

    def apply_from(vs, ref, r, n, center, we, ww, ws, wn, keep):
        last, start = masks(n)
        ve, vw = to_east(vs, last), to_west(vs, start)
        vs_, vn = rows_of(ref, r + 1, n), rows_of(ref, r - 1, n)
        return keep_in(
            [
                center[j] * vs[j] - ((ws[j] * vs_[j] + wn[j] * vn[j]) + (we[j] * ve[j] + ww[j] * vw[j]))
                for j in range(ext)
            ],
            keep,
        )

    def over_rows(step, accs):
        step(TOP - HALO, HALO, None, has_n)
        step(END, HALO, None, has_s)

        def loop(i, accs):
            return step(pl.multiple_of(TOP + i * STEP, STEP), STEP, accs, None)

        return lax.fori_loop(0, rows // STEP, loop, accs)

    def blank(k):
        return tuple(zero for _ in range(k))

    def pass1(r, n, accs, keep):
        last, start = masks(n)
        c0 = rows_of(C, r, n)
        cs, cn = rows_of(C, r + 1, n), rows_of(C, r - 1, n)
        ce, cw = to_east(c0, last), to_west(c0, start)
        we = [c0[j] + ce[j] for j in range(ext)]
        ww = [c0[j] + cw[j] for j in range(ext)]
        ws = [c0[j] + cs[j] for j in range(ext)]
        wn = [c0[j] + cn[j] for j in range(ext)]
        center = [(ws[j] + wn[j]) + (we[j] + ww[j]) for j in range(ext)]
        put(WE, r, n, we)
        put(WW, r, n, ww)
        put(WS, r, n, ws)
        put(CE, r, n, center)
        b = rows_of(B, r, n)
        v1 = apply_from(b, B, r, n, center, we, ww, ws, wn, keep)
        put(V1, r, n, v1)
        if accs is None:
            return None
        q = rows_of(Q, r, n)
        return add(accs, ((b, b), (b, v1), (v1, v1), (q, None), (q, b), (q, v1), (q, q)))

    nu0, nu1, nu2, s_q, s_qb, s_q1, mu0 = over_rows(pass1, blank(7))

    def weights_of(r, n):
        return rows_of(WE, r, n), rows_of(WW, r, n), rows_of(WS, r, n), rows_of(WS, r - 1, n)

    def pass2(r, n, accs, keep):
        v1 = rows_of(V1, r, n)
        v2 = apply_from(v1, V1, r, n, rows_of(CE, r, n), *weights_of(r, n), keep)
        put(V2, r, n, v2)
        if accs is None:
            return None
        q = rows_of(Q, r, n)
        return add(accs, ((v1, v2), (v2, v2), (q, v2)))

    nu3, nu4, s_q2 = over_rows(pass2, blank(3))

    def energy(V, center):
        def step(i, acc):
            r = pl.multiple_of(TOP + i * STEP, STEP)
            last, _ = masks(STEP)
            v = rows_of(V, r, STEP)
            ve = to_east(v, last)
            total = None
            for j in range(tiles):
                out = WE[j, pl.ds(r, STEP), :] * ve[j] + WS[j, pl.ds(r, STEP), :] * V[j, pl.ds(r + 1, STEP), :]
                t = v[j] * (center[j, pl.ds(r, STEP), :] * v[j] - (out + out))
                total = t if total is None else total + t
            return fold(acc, total)

        return lax.fori_loop(0, rows // STEP, step, zero)

    nu5 = energy(V2, CE)

    lane8 = lax.broadcasted_iota(jnp.int32, (8, LANE), 1)

    def start_stage(buf, stage, along_col):
        count, mine = (ncol, me_c) if along_col else (nrow, me_r)
        copies = []
        for d in range(1, count):
            to = lax.rem(mine + d, count)
            copy = pltpu.make_async_remote_copy(
                src_ref=buf.at[mine], dst_ref=buf.at[mine],
                send_sem=as_sem.at[stage, d], recv_sem=ar_sem.at[stage, d],
                device_id=(me_r, to) if along_col else (to, me_c), device_id_type=MESH,
            )
            copy.start()
            copies.append(copy)
        return copies

    def finish_stage(buf, copies):
        for copy in copies:
            copy.wait_recv()
        terms = [buf[k] for k in range(buf.shape[0])]
        while len(terms) > 1:
            terms = [terms[k] + terms[k + 1] if k + 1 < len(terms) else terms[k] for k in range(0, len(terms), 2)]
        return terms[0]

    def gather(accs):
        packed = jnp.zeros((8, LANE), jnp.float32)
        for k, acc in enumerate(accs):
            packed = jnp.where(lane8 == k, jnp.sum(acc, axis=1, keepdims=True), packed)
        return jnp.sum(packed, axis=0, keepdims=True)

    def spread(row, k):
        return jnp.broadcast_to(row[:, k : k + 1], (1, LANE))

    ga[me_c] = gather((nu0, nu1, nu2, nu3, nu4, nu5, s_q, s_qb, s_q1, s_q2))
    stage_a = start_stage(ga, 0, True)

    def pass_q(r, n, accs, keep):
        put(LP, r, n, apply_from(rows_of(Q, r, n), Q, r, n, rows_of(CE, r, n), *weights_of(r, n), keep))
        return accs

    over_rows(pass_q, 0)

    gb[me_r] = finish_stage(ga, stage_a)
    stage_b = start_stage(gb, 1, False)
    for copy in sends + stage_a:
        copy.wait_send()
    sums = finish_stage(gb, stage_b)

    c0, c1, c2 = solve([spread(sums, k) for k in range(6)])
    t_q, t_qb, t_q1, t_q2 = [spread(sums, k) for k in range(6, 10)]

    def pass_x(r, n, accs, keep):
        b, v1, v2 = rows_of(B, r, n), rows_of(V1, r, n), rows_of(V2, r, n)
        put(X, r, n, [c0 * b[j] + (c1 * v1[j] + c2 * v2[j]) for j in range(ext)])
        return accs

    over_rows(pass_x, 0)

    stores = []
    for j in range(tiles):
        copy = pltpu.make_async_copy(X.at[j, pl.ds(TOP, rows), :], tile_of(val_hbm, j), out_sem.at[0, j])
        copy.start()
        stores.append(copy)

    def pass3(r, n, accs, keep):
        last, start = masks(n)
        x = rows_of(X, r, n)
        xe, xw = to_east(x, last), to_west(x, start)
        xs, xn = rows_of(X, r + 1, n), rows_of(X, r - 1, n)
        q, lp, center = rows_of(Q, r, n), rows_of(LP, r, n), rows_of(CE, r, n)
        u1, full = [], []
        for j in range(ext):
            dr, dc = xs[j] - xn[j], xe[j] - xw[j]
            g = (0.25 / (2.0 * 0.25) * SCALE) * (dr * dr + dc * dc)
            full.append(center[j] + g)
            u1.append(lp[j] + g * q[j])
        u1 = keep_in(u1, keep)
        put(CE, r, n, full)
        put(U1, r, n, u1)
        if accs is None:
            return None
        return add(accs, ((q, u1), (u1, u1)))

    mu1, mu2 = over_rows(pass3, blank(2))

    def pass4(r, n, accs, keep):
        u1 = rows_of(U1, r, n)
        u2 = apply_from(u1, U1, r, n, rows_of(CE, r, n), *weights_of(r, n), keep)
        put(U2, r, n, u2)
        return None if accs is None else add(accs, ((u1, u2), (u2, u2)))

    mu3, mu4 = over_rows(pass4, blank(2))
    mu5 = energy(U2, CE)

    gc[me_c] = gather((mu0, mu1, mu2, mu3, mu4, mu5))
    stage_c = start_stage(gc, 2, True)
    erg_ref[...] = (t_qb - DISCOUNT * (c0 * t_qb + (c1 * t_q1 + c2 * t_q2))) / t_q
    for copy in stage_b:
        copy.wait_send()
    gd[me_r] = finish_stage(gc, stage_c)
    stage_d = start_stage(gd, 3, False)
    for copy in stage_c:
        copy.wait_send()
    for copy in stores:
        copy.wait()
    sums = finish_stage(gd, stage_d)
    d0, d1, d2 = solve([spread(sums, k) for k in range(6)])

    def last_pass(i, carry):
        r = pl.multiple_of(TOP + i * STEP, STEP)
        at = pl.ds(r, STEP)
        for j in range(tiles):
            Y[j, pl.ds(pl.multiple_of(i * STEP, STEP), STEP), :] = d0 * Q[j, at, :] + (d1 * U1[j, at, :] + d2 * U2[j, at, :])
        return carry

    lax.fori_loop(0, rows // STEP, last_pass, 0)
    outs = []
    for j in range(tiles):
        copy = pltpu.make_async_copy(Y.at[j], tile_of(den_hbm, j), out_sem.at[1, j])
        copy.start()
        outs.append(copy)
    for copy in stage_d:
        copy.wait_send()
    for copy in outs:
        copy.wait()


def solution(mesh):
    nrow, ncol = mesh.shape["row"], mesh.shape["col"]

    def body(running_cost, control_x, control_y, prior_density):
        rows, cols = running_cost.shape
        tiles = cols // LANE
        ext = tiles + 1
        pile = rows // 8
        big = pltpu.VMEM((ext, rows + 2 * TOP, LANE), jnp.float32)
        plain = pltpu.VMEM((tiles, rows, LANE), jnp.float32)
        most = max(nrow, ncol)
        value, density, ergodic = pl.pallas_call(
            functools.partial(kernel, nrow, ncol, rows, tiles),
            out_shape=(
                jax.ShapeDtypeStruct((rows, cols), jnp.float32),
                jax.ShapeDtypeStruct((rows, cols), jnp.float32),
                jax.ShapeDtypeStruct((1, LANE), jnp.float32),
            ),
            in_specs=[pl.BlockSpec(memory_space=pltpu.HBM)] * 4,
            out_specs=(
                pl.BlockSpec(memory_space=pltpu.HBM),
                pl.BlockSpec(memory_space=pltpu.HBM),
                pl.BlockSpec(memory_space=pltpu.VMEM),
            ),
            scratch_shapes=[plain] * 3
            + [big] * 13
            + [plain]
            + [pltpu.VMEM((pile, LANE), jnp.float32)] * 2
            + [pltpu.VMEM((pile + 16, LANE), jnp.float32)] * 2
            + [pltpu.VMEM((ncol, 1, LANE), jnp.float32), pltpu.VMEM((nrow, 1, LANE), jnp.float32)] * 2
            + [
                pltpu.SemaphoreType.DMA((4, tiles)),
                pltpu.SemaphoreType.DMA((2, tiles)),
                pltpu.SemaphoreType.DMA((12,)),
                pltpu.SemaphoreType.DMA((12,)),
                pltpu.SemaphoreType.DMA((4, most)),
                pltpu.SemaphoreType.DMA((4, most)),
            ],
            compiler_params=pltpu.CompilerParams(
                collective_id=0, has_side_effects=True, vmem_limit_bytes=48 * 1024 * 1024
            ),
        )(running_cost, control_x, control_y, prior_density)
        return value, density, ergodic[0, 0]

    spec = P("row", "col")
    return jax.shard_map(
        body,
        mesh=mesh,
        in_specs=(spec, spec, spec, spec),
        out_specs=(spec, spec, P()),
        check_vma=False,
    )
```

time: 336 us -> 54 us (0.16)
  starting transfers between devices: 121 us -> 0 us
  blocking collectives: 118 us -> 0 us
  Pallas kernels: 0 us -> 46.2 us
  other arithmetic: 31.9 us -> 0 us
  waiting for transfers between devices: 30.3 us -> 0 us
  between operations: 23.2 us -> 1.82 us
  local copies, waits for them, and re-layouts: 9.5 us -> 5.75 us
    all_to_all x9 -> x0, blocking collectives: 118 us -> none  [from_everyone(): lax.all_to_all(jnp.broadcast_to(shard[None], (count, *shard.shape)), axis...]
    ppermute x28 -> x0, starting transfers between devices: 75.5 us -> none  [the longest x14 53 us: padded_2(): lax.ppermute(last, axis, up)]
    pallas_call x0 -> x1, Pallas kernels: none -> 46.2 us  [body(): pl.pallas_call(functools.partial(kernel, nrow, ncol, rows, tiles), out_sh...]
    all_to_all x5 -> x0, starting transfers between devices: 45.5 us -> none  [from_everyone(): lax.all_to_all(jnp.broadcast_to(shard[None], (count, *shard.shape)), axis...]
    all_to_all x5 -> x0, waiting for transfers between devices: 22.9 us -> none  [from_everyone(): lax.all_to_all(jnp.broadcast_to(shard[None], (count, *shard.shape)), axis...]
    reduce_sum x22 -> x0, other arithmetic: 16.8 us -> none  [the longest x5 7.68 us: products(): jnp.sum(residual * residual)]
    concatenate x7 -> x0, other arithmetic: 9.58 us -> none  [together(): total = by_axis(jnp.concatenate([a.ravel() for a in arrays]), axis)]
    ppermute x28 -> x0, waiting for transfers between devices: 7.38 us -> none  [the longest x14 6.35 us: padded_2(): lax.ppermute(last, axis, up)]
  transfers between devices with their start and end apart: 33 -> 0, of which waited for: 9 -> 0; matrix products, arithmetic and copies ran while one was open for 4% -> 0% of each run, Pallas kernels for 0% -> 0%
where the time goes in v1:
time: 54 us; the launch traced here: 53.7 us
  Pallas kernels  46.2 us (86%)
  local copies, waits for them, and re-layouts  5.75 us (11%)
  between operations  1.82 us (3%)
    pallas_call x1, Pallas kernels, body(): pl.pallas_call(functools.partial(kernel, nrow, ncol, rows, tiles), out_sh...  46.2 us
    unnamed x10, local copies, waits for them, and re-layouts  5.75 us

profile of v1, /device:TPU:1, one launch (start us, length us, event | category | flops | bytes accessed | tf_op | source)
XLA Modules:
  0.0 53.7 jit_solution(10609212611597421310)
XLA Ops:
  0.6 0.0 copy-start
  0.6 1.0 %copy-done = f32[256,512]{1,0:T(8,128)S(1)} copy-done((f32[256,512]{1,0:T(8,128)S(1)}, f32[256,512]{1,0:T(8,128)}, u32[]{:S(2)}) %copy-start) | copy-done | bytes 524312
  1.7 0.0 copy-start.1
  1.7 1.0 %copy-done.1 = f32[256,512]{1,0:T(8,128)S(1)} copy-done((f32[256,512]{1,0:T(8,128)S(1)}, f32[256,512]{1,0:T(8,128)}, u32[]{:S(2)}) %copy-start.1) | copy-done | bytes 524312
  2.7 0.0 copy-start.2
  2.7 1.0 %copy-done.2 = f32[256,512]{1,0:T(8,128)S(1)} copy-done((f32[256,512]{1,0:T(8,128)S(1)}, f32[256,512]{1,0:T(8,128)}, u32[]{:S(2)}) %copy-start.2) | copy-done | bytes 524312
  3.8 0.0 copy-start.3
  3.8 1.0 %copy-done.3 = f32[256,512]{1,0:T(8,128)S(1)} copy-done((f32[256,512]{1,0:T(8,128)S(1)}, f32[256,512]{1,0:T(8,128)}, u32[]{:S(2)}) %copy-start.3) | copy-done | bytes 524312
  4.8 46.2 %shard_map.67 = (f32[256,512]{1,0:T(8,128)S(1)}, f32[256,512]{1,0:T(8,128)S(1)}, f32[1,128]{1,0:T(1,128)S(1)}) custom-call(f32[256,512]{1,0:T(8,128)S(1)} %copy-done, f32[256,512]{1,0:T(8,128)S(1)} %copy-done.1, f32[256,512]{1,0:T(8,128)S(1)} %copy-done.2, f32[256,512]{1,0:T(8,128)S(1)} %copy-done.3), custom_call_target="tpu_custom_call" | custom-call | tf_op jit(solution)/shard_map/pallas_call | solution.py:439
  51.0 0.8 %copy.10 = f32[256,512]{1,0:T(8,128)} copy(f32[256,512]{1,0:T(8,128)S(1)} %get-tuple-element.12) | data formatting | bytes 1048576
  51.8 0.8 %copy.11 = f32[256,512]{1,0:T(8,128)} copy(f32[256,512]{1,0:T(8,128)S(1)} %get-tuple-element.13) | data formatting | bytes 1048576
Async XLA Ops:
  0.6 1.0 %copy-start = (f32[256,512]{1,0:T(8,128)S(1)}, f32[256,512]{1,0:T(8,128)}, u32[]{:S(2)}) copy-start(f32[256,512]{1,0:T(8,128)} %rc_hbm.1) | copy-start | bytes 1572868
  1.7 1.0 %copy-start.1 = (f32[256,512]{1,0:T(8,128)S(1)}, f32[256,512]{1,0:T(8,128)}, u32[]{:S(2)}) copy-start(f32[256,512]{1,0:T(8,128)} %cx_hbm.1) | copy-start | bytes 1572868
  2.7 1.0 %copy-start.2 = (f32[256,512]{1,0:T(8,128)S(1)}, f32[256,512]{1,0:T(8,128)}, u32[]{:S(2)}) copy-start(f32[256,512]{1,0:T(8,128)} %cy_hbm.1) | copy-start | bytes 1572868
  3.8 1.0 %copy-start.3 = (f32[256,512]{1,0:T(8,128)S(1)}, f32[256,512]{1,0:T(8,128)}, u32[]{:S(2)}) copy-start(f32[256,512]{1,0:T(8,128)} %pr_hbm.1) | copy-start | bytes 1572868

commit v2 on v1

v2 whole, which is shorter than its diff:
```python
import functools

import jax
import jax.numpy as jnp
from jax import lax
from jax.experimental import pallas as pl
from jax.experimental.pallas import tpu as pltpu
from jax.sharding import PartitionSpec as P

MESH = pl.DeviceIdType.MESH

SCALE = 1.0 / 64.0
FACE = 0.25 * 0.5 * SCALE
DISCOUNT = 0.05

LANE = 128
TOP = 16
HALO = 8


def solve(nu):
    shift = DISCOUNT * SCALE
    m = [nu[k + 1] + shift * nu[k] for k in range(5)]
    l1 = m[1] / m[0]
    l2 = m[2] / m[0]
    d1 = m[2] - l1 * m[1]
    e = m[3] - l2 * m[1]
    l3 = e / d1
    d2 = (m[4] - l2 * m[2]) - l3 * e
    y0 = nu[0]
    y1 = nu[1] - l1 * y0
    y2 = (nu[2] - l2 * y0) - l3 * y1
    c2 = y2 / d2
    c1 = y1 / d1 - l3 * c2
    c0 = y0 / m[0] - l1 * c1 - l2 * c2
    return c0 * SCALE, c1 * SCALE, c2 * SCALE


def kernel(
    nrow, ncol, nx, rows, tiles, step_rows,
    rc_hbm, cx_hbm, cy_hbm, pr_hbm,
    val_ref, den_ref, erg_ref,
    cx, cy, rc, C, B, Q, WE, WW, WS, CE, V1, V2, X, LP, U1, U2,
    pack_e, pack_w, from_w, from_e, ga, gb, gc, gd,
    in_sem, hs_sem, hr_sem, as_sem, ar_sem, near_sem,
):
    me_r = lax.axis_index("row")
    me_c = lax.axis_index("col")
    up, down = lax.rem(me_r + nrow - 1, nrow), lax.rem(me_r + 1, nrow)
    west, east = lax.rem(me_c + ncol - 1, ncol), lax.rem(me_c + 1, ncol)
    ext = tiles + 1
    END = TOP + rows

    def tile_of(ref, j):
        return ref.at[:, pl.ds(j * LANE, LANE)]

    loads = {}
    for n, (src, dst, top) in enumerate(((cx_hbm, cx, 0), (cy_hbm, cy, 0), (rc_hbm, rc, 0), (pr_hbm, Q, TOP))):
        for j in range(tiles):
            copy = pltpu.make_async_copy(tile_of(src, j), dst.at[j, pl.ds(top, rows), :], in_sem.at[n, j])
            copy.start()
            loads[n, j] = copy

    nz, ny = nrow // 2, ncol // nx
    core, z = lax.rem(me_r, 2), me_r // 2
    x, y = me_c // ny, lax.rem(me_c, ny)

    def at_offset(dz, dc, dx, dy):
        r = 2 * lax.rem(z + dz, nz) + lax.rem(core + dc, 2)
        return r, ny * lax.rem(x + dx, nx) + lax.rem(y + dy, ny)

    def offsets(zs, cs, xs, ys):
        every = {(a % nz, b, c % nx, d % ny) for a in zs for b in cs for c in xs for d in ys}
        return sorted(every - {(0, 0, 0, 0)})

    def tell(sem, to):
        pl.semaphore_signal(sem, inc=1, device_id=to, device_id_type=MESH)

    not_first, not_last = me_r > 0, me_r < nrow - 1
    not_west, not_east = me_c > 0, me_c < ncol - 1
    beyond = me_r + 2 * core - 1
    far_row = lax.rem(beyond + nrow, nrow)

    def when(*conditions):
        def run(fn):
            for c in conditions[::-1]:
                fn = functools.partial(lambda c, f: pl.when(c)(f) and None, c, fn)
            fn()
        return run

    far_there = (beyond >= 0, beyond < nrow)

    barrier = pltpu.get_barrier_semaphore()
    around = (-1, 0, 1)
    near = offsets((0,), (0, 1), around, around) + offsets(around, (0,), (0,), (0,))
    for o in near:
        tell(barrier, at_offset(*o))
    when(*far_there)(lambda: tell(barrier, (far_row, me_c)))
    when(*far_there, not_west)(lambda: tell(barrier, (far_row, west)))
    when(*far_there, not_east)(lambda: tell(barrier, (far_row, east)))

    zero = jnp.zeros((8, LANE), jnp.float32)
    for ref in (C, B, Q, WS, V1, V2, X, U1, U2):
        for j in range(ext):
            ref[j, pl.ds(0, 8), :] = zero
            ref[j, pl.ds(END + HALO, 8), :] = zero

    low, high = pl.ds(0, 8), pl.ds(rows // 8 - 8, 8)
    sw_at, nw_at = pl.ds(rows // 8, 8), pl.ds(rows // 8 + 8, 8)

    @pl.when(me_c == 0)
    def _():
        from_w[...] = jnp.zeros_like(from_w)

    @pl.when(me_c == ncol - 1)
    def _():
        from_e[...] = jnp.zeros_like(from_e)

    def no_row(top, corner):
        for f in (C, B, Q):
            for j in range(tiles):
                f[j, pl.ds(top, HALO), :] = zero
        from_w[corner, :] = zero
        from_e[corner, :] = zero

    @pl.when(me_r == 0)
    def _():
        no_row(TOP - HALO, nw_at)

    @pl.when(me_r == nrow - 1)
    def _():
        no_row(END, sw_at)

    for copy in loads.values():
        copy.wait()

    def first(i, carry):
        r = pl.multiple_of(i * step_rows, step_rows)
        for j in range(tiles):
            a, b = cx[j, pl.ds(r, step_rows), :], cy[j, pl.ds(r, step_rows), :]
            cost = 0.5 * (a * a + b * b)
            C[j, pl.ds(TOP + r, step_rows), :] = (1.0 + cost) * FACE
            B[j, pl.ds(TOP + r, step_rows), :] = rc[j, pl.ds(r, step_rows), :] + cost
        return carry

    lax.fori_loop(0, rows // step_rows, first, 0)

    parts = LANE // 16
    pile = rows // parts
    lane = lax.broadcasted_iota(jnp.int32, (pile, LANE), 1)
    slot = lane & 15
    is_c, is_b = slot < 6, slot < 11
    acc_e = jnp.zeros((pile, LANE), jnp.float32)
    acc_w = jnp.zeros((pile, LANE), jnp.float32)
    for k in range(parts):
        at = pl.ds(TOP + pile * k, pile)
        here = (lane >> 4) == k
        got = []
        for j, firsts in ((tiles - 1, (122, 123, 125)), (0, (0, 0, 0))):
            rolled = [
                pltpu.roll(f[j, at, :], (16 * k + o - s) % LANE, 1)
                for f, o, s in zip((C, B, Q), (0, 6, 11), firsts)
            ]
            got.append(jnp.where(is_c, rolled[0], jnp.where(is_b, rolled[1], rolled[2])))
        acc_e = jnp.where(here, got[0], acc_e)
        acc_w = jnp.where(here, got[1], acc_w)
    pack_e[...] = acc_e
    pack_w[...] = acc_w

    any_west, any_east = (me_c + ncol - 1) // ncol, (2 * ncol - 2 - me_c) // ncol
    any_far = core * ((2 * nrow - 2 - me_r) // nrow) + (1 - core) * ((me_r + nrow - 1) // nrow)
    pl.semaphore_wait(barrier, len(near) + any_far * (1 + any_west + any_east))

    sends = []

    def send(src, dst, to, there, here):
        n = len(sends)
        copy = pltpu.make_async_remote_copy(
            src_ref=src, dst_ref=dst, send_sem=hs_sem.at[n], recv_sem=hr_sem.at[n],
            device_id=to, device_id_type=MESH,
        )
        when(*there)(copy.start)
        sends.append((copy, there, here))

    send(pack_e.at[high, :], from_w.at[nw_at, :], (down, east), (not_last, not_east), (not_first, not_west))
    send(pack_e.at[low, :], from_w.at[sw_at, :], (up, east), (not_first, not_east), (not_last, not_west))
    send(pack_w.at[high, :], from_e.at[nw_at, :], (down, west), (not_last, not_west), (not_first, not_east))
    send(pack_w.at[low, :], from_e.at[sw_at, :], (up, west), (not_first, not_west), (not_last, not_east))
    send(pack_e, from_w.at[pl.ds(0, pile), :], (me_r, east), (not_east,), (not_west,))
    send(pack_w, from_e.at[pl.ds(0, pile), :], (me_r, west), (not_west,), (not_east,))
    body = pl.ds(0, tiles)
    for f in (C, B, Q):
        send(f.at[body, pl.ds(TOP, HALO), :], f.at[body, pl.ds(END, HALO), :], (up, me_c), (not_first,), (not_last,))
        send(f.at[body, pl.ds(END - HALO, HALO), :], f.at[body, pl.ds(TOP - HALO, HALO), :], (down, me_c), (not_last,), (not_first,))

    first_ring = offsets((0,), (0,), around, around) + offsets(around, (0,), (0,), (0,))
    second_ring = offsets((-2, 2), (0,), (0,), (0,))
    for o in first_ring:
        tell(near_sem.at[0], at_offset(*o))

    for copy, _, here in sends:
        when(*here)(copy.wait_recv)

    pl.semaphore_wait(near_sem.at[0], len(first_ring))
    for o in second_ring:
        tell(near_sem.at[1], at_offset(*o))

    fone, fnil = jnp.float32(1.0), jnp.float32(0.0)
    has_n, has_s = jnp.where(not_first, fone, fnil), jnp.where(not_last, fone, fnil)
    has_w, has_e = jnp.where(not_west, fone, fnil), jnp.where(not_east, fone, fnil)

    def unpack(at, src, k, n):
        w, e = from_w[src, :], from_e[src, :]
        l = lax.broadcasted_iota(jnp.int32, (n, LANE), 1)
        none = jnp.zeros((n, LANE), jnp.float32)
        for f, o, s, wide in zip((C, B, Q), (0, 6, 11), (122, 123, 125), (6, 5, 3)):
            rw = pltpu.roll(w, (s - 16 * k - o) % LANE, 1)
            re = pltpu.roll(e, (-16 * k - o) % LANE, 1)
            f[tiles, at, :] = jnp.where(l >= s, rw, jnp.where(l < wide, re, none))

    for k in range(parts):
        unpack(pl.ds(TOP + pile * k, pile), pl.ds(0, pile), k, pile)
    unpack(pl.ds(TOP - HALO, HALO), nw_at, parts - 1, HALO)
    unpack(pl.ds(END, HALO), sw_at, 0, HALO)

    lane1 = lax.broadcasted_iota(jnp.int32, (1, LANE), 1)
    inside = jnp.where(lane1 < LANE // 2, has_e, has_w)

    def masks(n):
        l = lax.broadcasted_iota(jnp.int32, (n, LANE), 1)
        return l == LANE - 1, l == 0

    def to_east(vs, last):
        r = [pltpu.roll(v, LANE - 1, 1) for v in vs]
        return [jnp.where(last, r[(j + 1) % ext], r[j]) for j in range(ext)]

    def to_west(vs, start):
        r = [pltpu.roll(v, 1, 1) for v in vs]
        return [jnp.where(start, r[(j - 1) % ext], r[j]) for j in range(ext)]

    def rows_of(ref, r, n):
        return [ref[j, pl.ds(r, n), :] for j in range(ext)]

    def keep_in(vs, keep):
        vs = vs[:tiles] + [vs[tiles] * inside]
        return vs if keep is None else [v * keep for v in vs]

    def put(ref, r, n, vs):
        for j, v in enumerate(vs):
            ref[j, pl.ds(r, n), :] = v

    def fold(acc, v):
        while v.shape[0] > 8:
            half = v.shape[0] // 2
            v = v[:half, :] + v[half:, :]
        return acc + v

    def add(accs, lists):
        out = []
        for acc, (p, q) in zip(accs, lists):
            total = None
            for j in range(tiles):
                t = p[j] if q is None else p[j] * q[j]
                total = t if total is None else total + t
            out.append(fold(acc, total))
        return tuple(out)

    def apply_from(vs, ref, r, n, center, we, ww, ws, wn, keep):
        last, start = masks(n)
        ve, vw = to_east(vs, last), to_west(vs, start)
        vs_, vn = rows_of(ref, r + 1, n), rows_of(ref, r - 1, n)
        return keep_in(
            [
                center[j] * vs[j] - ((ws[j] * vs_[j] + wn[j] * vn[j]) + (we[j] * ve[j] + ww[j] * vw[j]))
                for j in range(ext)
            ],
            keep,
        )

    def over_rows(step, accs):
        step(TOP - HALO, HALO, None, has_n)
        step(END, HALO, None, has_s)

        def loop(i, accs):
            return step(pl.multiple_of(TOP + i * step_rows, TOP), step_rows, accs, None)

        return lax.fori_loop(0, rows // step_rows, loop, accs)

    def blank(k):
        return tuple(zero for _ in range(k))

    def pass1(r, n, accs, keep):
        last, start = masks(n)
        c0 = rows_of(C, r, n)
        cs, cn = rows_of(C, r + 1, n), rows_of(C, r - 1, n)
        ce, cw = to_east(c0, last), to_west(c0, start)
        we = [c0[j] + ce[j] for j in range(ext)]
        ww = [c0[j] + cw[j] for j in range(ext)]
        ws = [c0[j] + cs[j] for j in range(ext)]
        wn = [c0[j] + cn[j] for j in range(ext)]
        center = [(ws[j] + wn[j]) + (we[j] + ww[j]) for j in range(ext)]
        put(WE, r, n, we)
        put(WW, r, n, ww)
        put(WS, r, n, ws)
        put(CE, r, n, center)
        b = rows_of(B, r, n)
        v1 = apply_from(b, B, r, n, center, we, ww, ws, wn, keep)
        put(V1, r, n, v1)
        if accs is None:
            return None
        q = rows_of(Q, r, n)
        return add(accs, ((b, b), (b, v1), (v1, v1), (q, None), (q, b), (q, v1), (q, q)))

    nu0, nu1, nu2, s_q, s_qb, s_q1, mu0 = over_rows(pass1, blank(7))

    def weights_of(r, n):
        return rows_of(WE, r, n), rows_of(WW, r, n), rows_of(WS, r, n), rows_of(WS, r - 1, n)

    def pass2(r, n, accs, keep):
        v1 = rows_of(V1, r, n)
        v2 = apply_from(v1, V1, r, n, rows_of(CE, r, n), *weights_of(r, n), keep)
        put(V2, r, n, v2)
        if accs is None:
            return None
        q = rows_of(Q, r, n)
        return add(accs, ((v1, v2), (v2, v2), (q, v2)))

    nu3, nu4, s_q2 = over_rows(pass2, blank(3))

    def energy(V, center):
        def step(i, acc):
            r = pl.multiple_of(TOP + i * step_rows, TOP)
            last, _ = masks(step_rows)
            v = rows_of(V, r, step_rows)
            ve = to_east(v, last)
            total = None
            for j in range(tiles):
                out = WE[j, pl.ds(r, step_rows), :] * ve[j] + WS[j, pl.ds(r, step_rows), :] * V[j, pl.ds(r + 1, step_rows), :]
                t = v[j] * (center[j, pl.ds(r, step_rows), :] * v[j] - (out + out))
                total = t if total is None else total + t
            return fold(acc, total)

        return lax.fori_loop(0, rows // step_rows, step, zero)

    nu5 = energy(V2, CE)

    lane8 = lax.broadcasted_iota(jnp.int32, (8, LANE), 1)

    def add_up(buf, count):
        terms = [buf[k] for k in range(count)]
        while len(terms) > 1:
            terms = [terms[k] + terms[k + 1] if k + 1 < len(terms) else terms[k] for k in range(0, len(terms), 2)]
        return terms[0]

    def start_sum(part, ga, gb, stage):
        slot = core * ncol + me_c
        ga[slot] = part
        out = []
        for d in sorted(range(ncol), key=lambda d: -min(d, ncol - d)):
            copy = pltpu.make_async_remote_copy(
                src_ref=ga.at[slot], dst_ref=ga.at[slot],
                send_sem=as_sem.at[stage, d], recv_sem=ar_sem.at[stage, core * ncol + d],
                device_id=(2 * z + 1, lax.rem(me_c + d, ncol)), device_id_type=MESH,
            )
            if d == 0:
                pl.when(core == 0)(copy.start)
            else:
                copy.start()
            out.append((d, copy))
        return out

    def arrival(buf, slot, sem):
        return pltpu.make_async_remote_copy(
            src_ref=buf.at[slot], dst_ref=buf.at[slot], send_sem=sem, recv_sem=sem,
            device_id=(far_row, me_c), device_id_type=MESH,
        )

    def finish_sum(out, ga, gb, stage):
        again = []
        for dz in sorted(range(nz), key=lambda d: -min(d, nz - d)):
            for to_core in (0, 1):
                if dz or to_core == 0:
                    again.append(
                        pltpu.make_async_remote_copy(
                            src_ref=gb.at[z], dst_ref=gb.at[z],
                            send_sem=as_sem.at[stage + 1, 2 * dz + to_core], recv_sem=ar_sem.at[stage + 1, dz],
                            device_id=(2 * lax.rem(z + dz, nz) + to_core, me_c), device_id_type=MESH,
                        )
                    )

        @pl.when(core == 1)
        def _():
            for n in range(2 * ncol):
                if n != ncol:
                    arrival(ga, 0, ar_sem.at[stage, n]).wait_recv()
            if stage == 0:
                pl.semaphore_wait(near_sem.at[1], len(second_ring))
            gb[z] = add_up(ga, 2 * ncol)
            for copy in again:
                copy.start()

        if stage == 0:
            pl.when(core == 0)(lambda: pl.semaphore_wait(near_sem.at[1], len(second_ring)))
        for d, copy in out:
            if d == 0:
                pl.when(core == 0)(copy.wait_send)
            else:
                copy.wait_send()
        for dz in range(nz):
            come = arrival(gb, 0, ar_sem.at[stage + 1, dz])
            if dz == 0:
                pl.when(core == 0)(come.wait_recv)
            else:
                come.wait_recv()
        return add_up(gb, nz), again

    def settle(again):
        @pl.when(core == 1)
        def _():
            for copy in again:
                copy.wait_send()

    def gather(accs):
        packed = jnp.zeros((8, LANE), jnp.float32)
        for k, acc in enumerate(accs):
            packed = jnp.where(lane8 == k, jnp.sum(acc, axis=1, keepdims=True), packed)
        return jnp.sum(packed, axis=0, keepdims=True)

    def spread(row, k):
        return jnp.broadcast_to(row[:, k : k + 1], (1, LANE))

    out1 = start_sum(gather((nu0, nu1, nu2, nu3, nu4, nu5, s_q, s_qb, s_q1, s_q2)), ga, gb, 0)

    def pass_q(r, n, accs, keep):
        put(LP, r, n, apply_from(rows_of(Q, r, n), Q, r, n, rows_of(CE, r, n), *weights_of(r, n), keep))
        return accs

    over_rows(pass_q, 0)

    for copy, there, _ in sends:
        when(*there)(copy.wait_send)
    sums, again1 = finish_sum(out1, ga, gb, 0)

    c0, c1, c2 = solve([spread(sums, k) for k in range(6)])
    t_q, t_qb, t_q1, t_q2 = [spread(sums, k) for k in range(6, 10)]

    def pass_x(r, n, accs, keep):
        b, v1, v2 = rows_of(B, r, n), rows_of(V1, r, n), rows_of(V2, r, n)
        value = [c0 * b[j] + (c1 * v1[j] + c2 * v2[j]) for j in range(ext)]
        put(X, r, n, value)
        if keep is None:
            for j in range(tiles):
                val_ref[pl.ds(pl.multiple_of(r - TOP, 8), n), pl.ds(j * LANE, LANE)] = value[j]
        return accs

    over_rows(pass_x, 0)

    def pass3(r, n, accs, keep):
        last, start = masks(n)
        x = rows_of(X, r, n)
        xe, xw = to_east(x, last), to_west(x, start)
        xs, xn = rows_of(X, r + 1, n), rows_of(X, r - 1, n)
        q, lp, center = rows_of(Q, r, n), rows_of(LP, r, n), rows_of(CE, r, n)
        u1, full = [], []
        for j in range(ext):
            dr, dc = xs[j] - xn[j], xe[j] - xw[j]
            g = (0.25 / (2.0 * 0.25) * SCALE) * (dr * dr + dc * dc)
            full.append(center[j] + g)
            u1.append(lp[j] + g * q[j])
        u1 = keep_in(u1, keep)
        put(CE, r, n, full)
        put(U1, r, n, u1)
        if accs is None:
            return None
        return add(accs, ((q, u1), (u1, u1)))

    mu1, mu2 = over_rows(pass3, blank(2))

    def pass4(r, n, accs, keep):
        u1 = rows_of(U1, r, n)
        u2 = apply_from(u1, U1, r, n, rows_of(CE, r, n), *weights_of(r, n), keep)
        put(U2, r, n, u2)
        return None if accs is None else add(accs, ((u1, u2), (u2, u2)))

    mu3, mu4 = over_rows(pass4, blank(2))
    mu5 = energy(U2, CE)

    out2 = start_sum(gather((mu0, mu1, mu2, mu3, mu4, mu5)), gc, gd, 2)
    erg_ref[...] = (t_qb - DISCOUNT * (c0 * t_qb + (c1 * t_q1 + c2 * t_q2))) / t_q
    settle(again1)
    sums, again2 = finish_sum(out2, gc, gd, 2)
    d0, d1, d2 = solve([spread(sums, k) for k in range(6)])

    def last_pass(i, carry):
        r = pl.multiple_of(i * step_rows, step_rows)
        at = pl.ds(TOP + r, step_rows)
        for j in range(tiles):
            den_ref[pl.ds(r, step_rows), pl.ds(j * LANE, LANE)] = d0 * Q[j, at, :] + (d1 * U1[j, at, :] + d2 * U2[j, at, :])
        return carry

    lax.fori_loop(0, rows // step_rows, last_pass, 0)
    settle(again2)


def store_kernel(val_ref, den_ref, val_hbm, den_hbm, sem):
    copies = [pltpu.make_async_copy(val_ref, val_hbm, sem.at[0]), pltpu.make_async_copy(den_ref, den_hbm, sem.at[1])]
    for copy in copies:
        copy.start()
    for copy in copies:
        copy.wait()


def solution(mesh):
    nrow, ncol = mesh.shape["row"], mesh.shape["col"]

    def body(running_cost, control_x, control_y, prior_density):
        rows, cols = running_cost.shape
        tiles = cols // LANE
        ext = tiles + 1
        pile = rows // 8
        big = pltpu.VMEM((ext, rows + 2 * TOP, LANE), jnp.float32)
        plain = pltpu.VMEM((tiles, rows, LANE), jnp.float32)
        most = max(nrow, ncol)
        value, density, ergodic = pl.pallas_call(
            functools.partial(kernel, nrow, ncol, 4 if ncol % 4 == 0 else 1, rows, tiles, min(rows, 64)),
            out_shape=(
                jax.ShapeDtypeStruct((rows, cols), jnp.float32),
                jax.ShapeDtypeStruct((rows, cols), jnp.float32),
                jax.ShapeDtypeStruct((1, LANE), jnp.float32),
            ),
            in_specs=[pl.BlockSpec(memory_space=pltpu.HBM)] * 4,
            out_specs=(pl.BlockSpec(memory_space=pltpu.VMEM),) * 3,
            scratch_shapes=[plain] * 3
            + [big] * 13
            + [pltpu.VMEM((pile, LANE), jnp.float32)] * 2
            + [pltpu.VMEM((pile + 16, LANE), jnp.float32)] * 2
            + [pltpu.VMEM((2 * ncol, 1, LANE), jnp.float32), pltpu.VMEM((nrow // 2, 1, LANE), jnp.float32)] * 2
            + [
                pltpu.SemaphoreType.DMA((4, tiles)),
                pltpu.SemaphoreType.DMA((12,)),
                pltpu.SemaphoreType.DMA((12,)),
                pltpu.SemaphoreType.DMA((4, most)),
                pltpu.SemaphoreType.DMA((4, 2 * ncol)),
                pltpu.SemaphoreType.REGULAR((2,)),
            ],
            compiler_params=pltpu.CompilerParams(
                collective_id=0, has_side_effects=True, vmem_limit_bytes=55200000
            ),
        )(running_cost, control_x, control_y, prior_density)
        value, density = pl.pallas_call(
            store_kernel,
            out_shape=(jax.ShapeDtypeStruct((rows, cols), jnp.float32),) * 2,
            in_specs=[pl.BlockSpec(memory_space=pltpu.VMEM)] * 2,
            out_specs=(pl.BlockSpec(memory_space=pltpu.HBM),) * 2,
            scratch_shapes=[pltpu.SemaphoreType.DMA((2,))],
            compiler_params=pltpu.CompilerParams(vmem_limit_bytes=4 * 1024 * 1024),
        )(value, density)
        return value, density, ergodic[0, 0]

    spec = P("row", "col")
    return jax.shard_map(
        body,
        mesh=mesh,
        in_specs=(spec, spec, spec, spec),
        out_specs=(spec, spec, P()),
        check_vma=False,
    )
```

time: 54 us -> 40 us (0.74)
  Pallas kernels: 46.2 us -> 38 us
  local copies, waits for them, and re-layouts: 5.75 us -> 0 us
    pallas_call x1 -> x2, Pallas kernels: 46.2 us -> 38 us  [the longest x1 37 us: body(): pl.pallas_call(functools.partial(kernel, nrow, ncol, 4 if ncol % 4 == 0 e...]
    unnamed x10 -> x0, local copies, waits for them, and re-layouts: 5.75 us -> none
where the time goes in v2:
time: 40 us; the launch traced here: 39.8 us
  Pallas kernels  38 us (95%)
  between operations  1.8 us (4%)
    pallas_call x1, Pallas kernels, body(): pl.pallas_call(functools.partial(kernel, nrow, ncol, 4 if ncol % 4 == 0 e...  37 us
    pallas_call x1, Pallas kernels, body(): pl.pallas_call(store_kernel, out_shape=(jax.ShapeDtypeStruct((rows, cols)...  0.99 us

profile of v2, /device:TPU:1, one launch (start us, length us, event | category | flops | bytes accessed | tf_op | source)
XLA Modules:
  0.0 39.8 jit_solution(7116440226159208905)
XLA Ops:
  0.6 37.0 %shard_map.67 = (f32[256,512]{1,0:T(8,128)S(1)}, f32[256,512]{1,0:T(8,128)S(1)}, f32[1,128]{1,0:T(1,128)S(1)}) custom-call(f32[256,512]{1,0:T(8,128)} %rc_hbm.1, f32[256,512]{1,0:T(8,128)} %cx_hbm.1, f32[256,512]{1,0:T(8,128)} %cy_hbm.1, f32[256,512]{1,0:T(8,128)} %pr_hbm.1), custom_call_target="tpu_custom_call" | custom-call | tf_op jit(solution)/shard_map/pallas_call | solution.py:524
  37.7 1.0 %shard_map.68 = (f32[256,512]{1,0:T(8,128)}, f32[256,512]{1,0:T(8,128)}) custom-call(f32[256,512]{1,0:T(8,128)S(1)} %get-tuple-element.8.val_ref, f32[256,512]{1,0:T(8,128)S(1)} %get-tuple-element.9.den_ref), custom_call_target="tpu_custom_call" | custom-call | tf_op jit(solution)/shard_map/pallas_call | solution.py:550

commit v3 on v2

--- a/solution.py
+++ b/solution.py
@@ -41,7 +41,7 @@
     rc_hbm, cx_hbm, cy_hbm, pr_hbm,
     val_ref, den_ref, erg_ref,
     cx, cy, rc, C, B, Q, WE, WW, WS, CE, V1, V2, X, LP, U1, U2,
-    pack_e, pack_w, from_w, from_e, ga, gb, gc, gd,
+    pack_e, pack_w, from_w, from_e, SC, SB, S1, S2, ga, gb, gc, gd,
     in_sem, hs_sem, hr_sem, as_sem, ar_sem, near_sem,
 ):
     me_r = lax.axis_index("row")
@@ -134,16 +134,34 @@
     for copy in loads.values():
         copy.wait()
 
-    def first(i, carry):
+    def fold(acc, v):
+        while v.shape[0] > 8:
+            n = v.shape[0]
+            if n % 16 == 0:
+                v = v[: n // 2, :] + v[n // 2 :, :]
+            else:
+                acc, v = acc + v[n - 8 :, :], v[: n - 8, :]
+        return acc + v
+
+    def blank(k):
+        return tuple(zero for _ in range(k))
+
+    def first(i, accs):
         r = pl.multiple_of(i * step_rows, step_rows)
+        at = pl.ds(TOP + r, step_rows)
+        terms = [None] * 4
         for j in range(tiles):
             a, b = cx[j, pl.ds(r, step_rows), :], cy[j, pl.ds(r, step_rows), :]
             cost = 0.5 * (a * a + b * b)
-            C[j, pl.ds(TOP + r, step_rows), :] = (1.0 + cost) * FACE
-            B[j, pl.ds(TOP + r, step_rows), :] = rc[j, pl.ds(r, step_rows), :] + cost
-        return carry
-
-    lax.fori_loop(0, rows // step_rows, first, 0)
+            force = rc[j, pl.ds(r, step_rows), :] + cost
+            C[j, at, :] = (1.0 + cost) * FACE
+            B[j, at, :] = force
+            q = Q[j, at, :]
+            for k, t in enumerate((force * force, q, q * force, q * q)):
+                terms[k] = t if j == 0 else terms[k] + t
+        return tuple(fold(acc, t) for acc, t in zip(accs, terms))
+
+    nu0, s_q, s_qb, mu0 = lax.fori_loop(0, rows // step_rows, first, blank(4))
 
     parts = LANE // 16
     pile = rows // parts
@@ -198,31 +216,9 @@
     for o in first_ring:
         tell(near_sem.at[0], at_offset(*o))
 
-    for copy, _, here in sends:
-        when(*here)(copy.wait_recv)
-
-    pl.semaphore_wait(near_sem.at[0], len(first_ring))
-    for o in second_ring:
-        tell(near_sem.at[1], at_offset(*o))
-
     fone, fnil = jnp.float32(1.0), jnp.float32(0.0)
     has_n, has_s = jnp.where(not_first, fone, fnil), jnp.where(not_last, fone, fnil)
     has_w, has_e = jnp.where(not_west, fone, fnil), jnp.where(not_east, fone, fnil)
-
-    def unpack(at, src, k, n):
-        w, e = from_w[src, :], from_e[src, :]
-        l = lax.broadcasted_iota(jnp.int32, (n, LANE), 1)
-        none = jnp.zeros((n, LANE), jnp.float32)
-        for f, o, s, wide in zip((C, B, Q), (0, 6, 11), (122, 123, 125), (6, 5, 3)):
-            rw = pltpu.roll(w, (s - 16 * k - o) % LANE, 1)
-            re = pltpu.roll(e, (-16 * k - o) % LANE, 1)
-            f[tiles, at, :] = jnp.where(l >= s, rw, jnp.where(l < wide, re, none))
-
-    for k in range(parts):
-        unpack(pl.ds(TOP + pile * k, pile), pl.ds(0, pile), k, pile)
-    unpack(pl.ds(TOP - HALO, HALO), nw_at, parts - 1, HALO)
-    unpack(pl.ds(END, HALO), sw_at, 0, HALO)
-
     lane1 = lax.broadcasted_iota(jnp.int32, (1, LANE), 1)
     inside = jnp.where(lane1 < LANE // 2, has_e, has_w)
 
@@ -232,47 +228,45 @@
 
     def to_east(vs, last):
         r = [pltpu.roll(v, LANE - 1, 1) for v in vs]
-        return [jnp.where(last, r[(j + 1) % ext], r[j]) for j in range(ext)]
+        return [jnp.where(last, r[(j + 1) % len(vs)], r[j]) for j in range(len(vs))]
 
     def to_west(vs, start):
         r = [pltpu.roll(v, 1, 1) for v in vs]
-        return [jnp.where(start, r[(j - 1) % ext], r[j]) for j in range(ext)]
-
-    def rows_of(ref, r, n):
-        return [ref[j, pl.ds(r, n), :] for j in range(ext)]
+        return [jnp.where(start, r[(j - 1) % len(vs)], r[j]) for j in range(len(vs))]
+
+    def rows_of(ref, r, n, count=ext):
+        return [ref[j, pl.ds(r, n), :] for j in range(count)]
 
     def keep_in(vs, keep):
-        vs = vs[:tiles] + [vs[tiles] * inside]
+        if len(vs) == ext:
+            vs = vs[:tiles] + [vs[tiles] * inside]
         return vs if keep is None else [v * keep for v in vs]
 
     def put(ref, r, n, vs):
         for j, v in enumerate(vs):
             ref[j, pl.ds(r, n), :] = v
 
-    def fold(acc, v):
-        while v.shape[0] > 8:
-            half = v.shape[0] // 2
-            v = v[:half, :] + v[half:, :]
-        return acc + v
-
-    def add(accs, lists):
+    def add(accs, lists, weigh=None):
         out = []
         for acc, (p, q) in zip(accs, lists):
             total = None
             for j in range(tiles):
-                t = p[j] if q is None else p[j] * q[j]
+                t = p[j] * q[j]
+                if weigh is not None and weigh[j] is not None:
+                    t = t * weigh[j]
                 total = t if total is None else total + t
             out.append(fold(acc, total))
         return tuple(out)
 
     def apply_from(vs, ref, r, n, center, we, ww, ws, wn, keep):
+        count = len(vs)
         last, start = masks(n)
         ve, vw = to_east(vs, last), to_west(vs, start)
-        vs_, vn = rows_of(ref, r + 1, n), rows_of(ref, r - 1, n)
+        vs_, vn = rows_of(ref, r + 1, n, count), rows_of(ref, r - 1, n, count)
         return keep_in(
             [
                 center[j] * vs[j] - ((ws[j] * vs_[j] + wn[j] * vn[j]) + (we[j] * ve[j] + ww[j] * vw[j]))
-                for j in range(ext)
+                for j in range(count)
             ],
             keep,
         )
@@ -286,63 +280,168 @@
 
         return lax.fori_loop(0, rows // step_rows, loop, accs)
 
-    def blank(k):
-        return tuple(zero for _ in range(k))
-
-    def pass1(r, n, accs, keep):
+    def weights_and_v1(r, n, count, keep):
         last, start = masks(n)
-        c0 = rows_of(C, r, n)
-        cs, cn = rows_of(C, r + 1, n), rows_of(C, r - 1, n)
+        c0 = rows_of(C, r, n, count)
+        cs, cn = rows_of(C, r + 1, n, count), rows_of(C, r - 1, n, count)
         ce, cw = to_east(c0, last), to_west(c0, start)
-        we = [c0[j] + ce[j] for j in range(ext)]
-        ww = [c0[j] + cw[j] for j in range(ext)]
-        ws = [c0[j] + cs[j] for j in range(ext)]
-        wn = [c0[j] + cn[j] for j in range(ext)]
-        center = [(ws[j] + wn[j]) + (we[j] + ww[j]) for j in range(ext)]
+        we = [c0[j] + ce[j] for j in range(count)]
+        ww = [c0[j] + cw[j] for j in range(count)]
+        ws = [c0[j] + cs[j] for j in range(count)]
+        wn = [c0[j] + cn[j] for j in range(count)]
+        center = [(ws[j] + wn[j]) + (we[j] + ww[j]) for j in range(count)]
         put(WE, r, n, we)
         put(WW, r, n, ww)
         put(WS, r, n, ws)
         put(CE, r, n, center)
-        b = rows_of(B, r, n)
-        v1 = apply_from(b, B, r, n, center, we, ww, ws, wn, keep)
+        v1 = apply_from(rows_of(B, r, n, count), B, r, n, center, we, ww, ws, wn, keep)
         put(V1, r, n, v1)
+        return v1
+
+    def weights_of(r, n, count=ext):
+        return rows_of(WE, r, n, count), rows_of(WW, r, n, count), rows_of(WS, r, n, count), rows_of(WS, r - 1, n, count)
+
+    def second(r, n, count, keep):
+        v1 = rows_of(V1, r, n, count)
+        v2 = apply_from(v1, V1, r, n, rows_of(CE, r, n, count), *weights_of(r, n, count), keep)
+        put(V2, r, n, v2)
+        return v1, v2
+
+    def face_terms(V, r, n, count, weigh=None):
+        last, _ = masks(n)
+        v = rows_of(V, r, n, count)
+        ve = to_east(v, last)
+        total = None
+        for j in range(tiles):
+            out = WE[j, pl.ds(r, n), :] * ve[j] + WS[j, pl.ds(r, n), :] * V[j, pl.ds(r + 1, n), :]
+            t = v[j] * (CE[j, pl.ds(r, n), :] * v[j] - (out + out))
+            if weigh is not None and weigh[j] is not None:
+                t = t * weigh[j]
+            total = t if total is None else total + t
+        return total
+
+    in_west = jnp.where(lane1 >= 6, jnp.ones((1, LANE), jnp.float32), jnp.zeros((1, LANE), jnp.float32))
+    in_east = jnp.where(lane1 < LANE - 6, jnp.ones((1, LANE), jnp.float32), jnp.zeros((1, LANE), jnp.float32))
+    weigh = [None] * tiles
+    weigh[0] = in_west
+    weigh[tiles - 1] = in_east if tiles > 1 else in_west * in_east
+    INNER = 16
+    part = (rows - 2 * INNER) // 4
+
+    def over_center(step, accs):
+        step(TOP + 8, 8, None)
+        step(END - 16, 8, None)
+
+        def loop(i, accs):
+            return step(pl.multiple_of(TOP + INNER + i * part, 8), part, accs)
+
+        return lax.fori_loop(0, 4, loop, accs)
+
+    def center1(r, n, accs):
+        v1 = weights_and_v1(r, n, tiles, None)
         if accs is None:
             return None
-        q = rows_of(Q, r, n)
-        return add(accs, ((b, b), (b, v1), (v1, v1), (q, None), (q, b), (q, v1), (q, q)))
-
-    nu0, nu1, nu2, s_q, s_qb, s_q1, mu0 = over_rows(pass1, blank(7))
-
-    def weights_of(r, n):
-        return rows_of(WE, r, n), rows_of(WW, r, n), rows_of(WS, r, n), rows_of(WS, r - 1, n)
-
-    def pass2(r, n, accs, keep):
-        v1 = rows_of(V1, r, n)
-        v2 = apply_from(v1, V1, r, n, rows_of(CE, r, n), *weights_of(r, n), keep)
-        put(V2, r, n, v2)
+        return add(accs, ((rows_of(B, r, n, tiles), v1), (v1, v1), (rows_of(Q, r, n, tiles), v1)), weigh)
+
+    def center2(r, n, accs):
+        v1, v2 = second(r, n, tiles, None)
         if accs is None:
             return None
-        q = rows_of(Q, r, n)
-        return add(accs, ((v1, v2), (v2, v2), (q, v2)))
-
-    nu3, nu4, s_q2 = over_rows(pass2, blank(3))
-
-    def energy(V, center):
-        def step(i, acc):
-            r = pl.multiple_of(TOP + i * step_rows, TOP)
-            last, _ = masks(step_rows)
-            v = rows_of(V, r, step_rows)
-            ve = to_east(v, last)
-            total = None
-            for j in range(tiles):
-                out = WE[j, pl.ds(r, step_rows), :] * ve[j] + WS[j, pl.ds(r, step_rows), :] * V[j, pl.ds(r + 1, step_rows), :]
-                t = v[j] * (center[j, pl.ds(r, step_rows), :] * v[j] - (out + out))
-                total = t if total is None else total + t
-            return fold(acc, total)
-
-        return lax.fori_loop(0, rows // step_rows, step, zero)
-
-    nu5 = energy(V2, CE)
+        return add(accs, ((v1, v2), (v2, v2), (rows_of(Q, r, n, tiles), v2)), weigh)
+
+    def center3(i, acc):
+        return fold(acc, face_terms(V2, pl.multiple_of(TOP + INNER + i * part, 8), part, tiles, weigh))
+
+    nu1, nu2, s_q1 = over_center(center1, blank(3))
+    nu3, nu4, s_q2 = over_center(center2, blank(3))
+    nu5 = lax.fori_loop(0, 4, center3, zero)
+
+    def own_columns(f, j, shift):
+        acc = jnp.zeros((pile, LANE), jnp.float32)
+        for k in range(parts):
+            acc = jnp.where((lane >> 4) == k, pltpu.roll(f[j, pl.ds(TOP + pile * k, pile), :], (16 * k + shift) % LANE, 1), acc)
+        return acc
+
+    own_w = [own_columns(f, 0, 6) for f in (C, B, Q)]
+    own_e = [own_columns(f, tiles - 1, 10 - LANE) for f in (C, B, Q)]
+
+    for copy, _, here in sends[:10]:
+        when(*here)(copy.wait_recv)
+
+    pl.semaphore_wait(near_sem.at[0], len(first_ring))
+    for o in second_ring:
+        tell(near_sem.at[1], at_offset(*o))
+
+    def unpack(at, src, k, n, fields):
+        w, e = from_w[src, :], from_e[src, :]
+        l = lax.broadcasted_iota(jnp.int32, (n, LANE), 1)
+        none = jnp.zeros((n, LANE), jnp.float32)
+        for f, o, s, wide in zip((C, B, Q)[:fields], (0, 6, 11), (122, 123, 125), (6, 5, 3)):
+            rw = pltpu.roll(w, (s - 16 * k - o) % LANE, 1)
+            re = pltpu.roll(e, (-16 * k - o) % LANE, 1)
+            f[tiles, at, :] = jnp.where(l >= s, rw, jnp.where(l < wide, re, none))
+
+    top_at, end_at = pl.ds(TOP - HALO, HALO), pl.ds(END, HALO)
+    for k in range(parts):
+        if pile * k < 32 or pile * (k + 1) > rows - 32:
+            unpack(pl.ds(TOP + pile * k, pile), pl.ds(0, pile), k, pile, 2)
+    unpack(top_at, nw_at, parts - 1, HALO, 2)
+    unpack(end_at, sw_at, 0, HALO, 2)
+
+    rows32 = lax.broadcasted_iota(jnp.int32, (32, LANE), 0)
+    ones32 = jnp.ones((32, LANE), jnp.float32)
+    tops = ((TOP - HALO, jnp.where(rows32 < HALO, has_n * ones32, ones32), HALO), (END - 24, jnp.where(rows32 >= 24, has_s * ones32, ones32), HALO))
+    def own_16(vs, skip):
+        return [v[skip : skip + 16, :] for v in vs]
+
+    for r, keep, skip in tops:
+        v1 = own_16(weights_and_v1(r, 32, ext, keep), skip)
+        b, q = rows_of(B, r + skip, 16, tiles), rows_of(Q, r + skip, 16, tiles)
+        nu1, nu2, s_q1 = add((nu1, nu2, s_q1), ((b, v1), (v1, v1), (q, v1)))
+    for r, keep, skip in tops:
+        v1, v2 = [own_16(v, skip) for v in second(r, 32, ext, keep)]
+        q = rows_of(Q, r + skip, 16, tiles)
+        nu3, nu4, s_q2 = add((nu3, nu4, s_q2), ((v1, v2), (v2, v2), (q, v2)))
+    for r, keep, skip in tops:
+        nu5 = fold(nu5, face_terms(V2, r + skip, 16, ext))
+
+    def put_strip(ref, n, v):
+        ref[n, pl.ds(8, pile), :] = v
+        ref[n, pl.ds(7, 1), :] = pltpu.roll(v[pile - 1 :, :], 16, 1)
+        ref[n, pl.ds(8 + pile, 1), :] = pltpu.roll(v[:1, :], LANE - 16, 1)
+
+    def below_above(ref, n):
+        return ref[n, pl.ds(9, pile), :], ref[n, pl.ds(7, pile), :]
+
+    sides = ((own_w, from_w, (0, -5), slot < 6, has_w, 6), (own_e, from_e, (10, 4), slot >= 10, has_e, 4))
+    row_at = lax.broadcasted_iota(jnp.int32, (pile, LANE), 0) + pile * (lane >> 4)
+    for n, (own, come, shifts, outer, there, begin) in enumerate(sides):
+        got = come[pl.ds(0, pile), :]
+        keep = jnp.where(outer, there * jnp.ones((pile, LANE), jnp.float32), jnp.ones((pile, LANE), jnp.float32))
+        middle = (row_at >= INNER) & (row_at < rows - INNER) & (slot >= begin) & (slot < begin + 6)
+        mine = jnp.where(middle, jnp.ones((pile, LANE), jnp.float32), jnp.zeros((pile, LANE), jnp.float32))
+        c, b = [jnp.where(outer, pltpu.roll(got, h % LANE, 1), o) for h, o in zip(shifts, own)]
+        q = own[2] * mine
+        put_strip(SC, n, c)
+        put_strip(SB, n, b)
+        c_s, c_n = below_above(SC, n)
+        we, ww, ws, wn = c + pltpu.roll(c, LANE - 1, 1), c + pltpu.roll(c, 1, 1), c + c_s, c + c_n
+        mid = (ws + wn) + (we + ww)
+
+        def strip_apply(ref, v):
+            put_strip(ref, n, v)
+            v_s, v_n = below_above(ref, n)
+            beside = we * pltpu.roll(v, LANE - 1, 1) + ww * pltpu.roll(v, 1, 1)
+            return (mid * v - ((ws * v_s + wn * v_n) + beside)) * keep
+
+        v1 = strip_apply(SB, b)
+        v2 = strip_apply(S1, v1)
+        put_strip(S2, n, v2)
+        out = we * pltpu.roll(v2, LANE - 1, 1) + ws * S2[n, pl.ds(9, pile), :]
+        m1, m2 = v1 * mine, v2 * mine
+        nu1, nu2, nu3 = fold(nu1, b * m1), fold(nu2, v1 * m1), fold(nu3, v1 * m2)
+        nu4, nu5 = fold(nu4, v2 * m2), fold(nu5, m2 * (mid * v2 - (out + out)))
+        s_q1, s_q2 = fold(s_q1, q * v1), fold(s_q2, q * v2)
 
     lane8 = lax.broadcasted_iota(jnp.int32, (8, LANE), 1)
 
@@ -431,10 +530,27 @@
 
     out1 = start_sum(gather((nu0, nu1, nu2, nu3, nu4, nu5, s_q, s_qb, s_q1, s_q2)), ga, gb, 0)
 
+    for copy, _, here in sends[10:]:
+        when(*here)(copy.wait_recv)
+    for k in range(parts):
+        unpack(pl.ds(TOP + pile * k, pile), pl.ds(0, pile), k, pile, 3)
+    unpack(top_at, nw_at, parts - 1, HALO, 3)
+    unpack(end_at, sw_at, 0, HALO, 3)
+
+    def all1(r, n, accs, keep):
+        weights_and_v1(r, n, ext, keep)
+        return accs
+
+    def all2(r, n, accs, keep):
+        second(r, n, ext, keep)
+        return accs
+
     def pass_q(r, n, accs, keep):
         put(LP, r, n, apply_from(rows_of(Q, r, n), Q, r, n, rows_of(CE, r, n), *weights_of(r, n), keep))
         return accs
 
+    over_rows(all1, 0)
+    over_rows(all2, 0)
     over_rows(pass_q, 0)
 
     for copy, there, _ in sends:
@@ -483,7 +599,12 @@
         return None if accs is None else add(accs, ((u1, u2), (u2, u2)))
 
     mu3, mu4 = over_rows(pass4, blank(2))
-    mu5 = energy(U2, CE)
+
+    def pass5(i, acc):
+        return fold(acc, face_terms(U2, pl.multiple_of(TOP + i * step_rows, TOP), step_rows, ext))
+
+    mu5 = lax.fori_loop(0, rows // step_rows, pass5, zero)
+
 
     out2 = start_sum(gather((mu0, mu1, mu2, mu3, mu4, mu5)), gc, gd, 2)
     erg_ref[...] = (t_qb - DISCOUNT * (c0 * t_qb + (c1 * t_q1 + c2 * t_q2))) / t_q
@@ -534,6 +655,7 @@
             + [big] * 13
             + [pltpu.VMEM((pile, LANE), jnp.float32)] * 2
             + [pltpu.VMEM((pile + 16, LANE), jnp.float32)] * 2
+            + [pltpu.VMEM((2, pile + 16, LANE), jnp.float32)] * 4
             + [pltpu.VMEM((2 * ncol, 1, LANE), jnp.float32), pltpu.VMEM((nrow // 2, 1, LANE), jnp.float32)] * 2
             + [
                 pltpu.SemaphoreType.DMA((4, tiles)),

time: 40 us -> 37.7 us (0.943)
  Pallas kernels: 38 us -> 35.7 us
    pallas_call x1, Pallas kernels: 37 us -> 34.7 us  [body(): pl.pallas_call(functools.partial(kernel, nrow, ncol, 4 if ncol % 4 == 0 e...]
where the time goes in v3:
time: 37.7 us; the launch traced here: 37.5 us
  Pallas kernels  35.7 us (95%)
  between operations  1.8 us (5%)
    pallas_call x1, Pallas kernels, body(): pl.pallas_call(functools.partial(kernel, nrow, ncol, 4 if ncol % 4 == 0 e...  34.7 us
    pallas_call x1, Pallas kernels, body(): pl.pallas_call(store_kernel, out_shape=(jax.ShapeDtypeStruct((rows, cols)...  0.99 us

profile of v3, /device:TPU:1, one launch (start us, length us, event | category | flops | bytes accessed | tf_op | source)
XLA Modules:
  0.0 37.5 jit_solution(17230361041491871735)
XLA Ops:
  0.6 34.7 %shard_map.67 = (f32[256,512]{1,0:T(8,128)S(1)}, f32[256,512]{1,0:T(8,128)S(1)}, f32[1,128]{1,0:T(1,128)S(1)}) custom-call(f32[256,512]{1,0:T(8,128)} %rc_hbm.1, f32[256,512]{1,0:T(8,128)} %cx_hbm.1, f32[256,512]{1,0:T(8,128)} %cy_hbm.1, f32[256,512]{1,0:T(8,128)} %pr_hbm.1), custom_call_target="tpu_custom_call" | custom-call | tf_op jit(solution)/shard_map/pallas_call | solution.py:645
  35.4 1.0 %shard_map.68 = (f32[256,512]{1,0:T(8,128)}, f32[256,512]{1,0:T(8,128)}) custom-call(f32[256,512]{1,0:T(8,128)S(1)} %get-tuple-element.8.val_ref, f32[256,512]{1,0:T(8,128)S(1)} %get-tuple-element.9.den_ref), custom_call_target="tpu_custom_call" | custom-call | tf_op jit(solution)/shard_map/pallas_call | solution.py:672

commit v4 on v3

--- a/solution.py
+++ b/solution.py
@@ -271,8 +271,9 @@
             keep,
         )
 
-    def over_rows(step, accs):
-        step(TOP - HALO, HALO, None, has_n)
+    def over_rows(step, accs, above=True):
+        if above:
+            step(TOP - HALO, HALO, None, has_n)
         step(END, HALO, None, has_s)
 
         def loop(i, accs):
@@ -326,7 +327,8 @@
     weigh[0] = in_west
     weigh[tiles - 1] = in_east if tiles > 1 else in_west * in_east
     INNER = 16
-    part = (rows - 2 * INNER) // 4
+    pieces = 2
+    part = (rows - 2 * INNER) // pieces
 
     def over_center(step, accs):
         step(TOP + 8, 8, None)
@@ -335,7 +337,7 @@
         def loop(i, accs):
             return step(pl.multiple_of(TOP + INNER + i * part, 8), part, accs)
 
-        return lax.fori_loop(0, 4, loop, accs)
+        return lax.fori_loop(0, pieces, loop, accs)
 
     def center1(r, n, accs):
         v1 = weights_and_v1(r, n, tiles, None)
@@ -354,7 +356,7 @@
 
     nu1, nu2, s_q1 = over_center(center1, blank(3))
     nu3, nu4, s_q2 = over_center(center2, blank(3))
-    nu5 = lax.fori_loop(0, 4, center3, zero)
+    nu5 = lax.fori_loop(0, pieces, center3, zero)
 
     def own_columns(f, j, shift):
         acc = jnp.zeros((pile, LANE), jnp.float32)
@@ -454,70 +456,51 @@
     def start_sum(part, ga, gb, stage):
         slot = core * ncol + me_c
         ga[slot] = part
-        out = []
         for d in sorted(range(ncol), key=lambda d: -min(d, ncol - d)):
             copy = pltpu.make_async_remote_copy(
-                src_ref=ga.at[slot], dst_ref=ga.at[slot],
-                send_sem=as_sem.at[stage, d], recv_sem=ar_sem.at[stage, core * ncol + d],
+                src_ref=ga.at[slot], dst_ref=ga.at[slot], send_sem=as_sem.at[stage], recv_sem=ar_sem.at[stage],
                 device_id=(2 * z + 1, lax.rem(me_c + d, ncol)), device_id_type=MESH,
             )
             if d == 0:
                 pl.when(core == 0)(copy.start)
             else:
                 copy.start()
-            out.append((d, copy))
-        return out
-
-    def arrival(buf, slot, sem):
-        return pltpu.make_async_remote_copy(
-            src_ref=buf.at[slot], dst_ref=buf.at[slot], send_sem=sem, recv_sem=sem,
-            device_id=(far_row, me_c), device_id_type=MESH,
-        )
-
-    def finish_sum(out, ga, gb, stage):
-        again = []
-        for dz in sorted(range(nz), key=lambda d: -min(d, nz - d)):
-            for to_core in (0, 1):
-                if dz or to_core == 0:
-                    again.append(
-                        pltpu.make_async_remote_copy(
-                            src_ref=gb.at[z], dst_ref=gb.at[z],
-                            send_sem=as_sem.at[stage + 1, 2 * dz + to_core], recv_sem=ar_sem.at[stage + 1, dz],
-                            device_id=(2 * lax.rem(z + dz, nz) + to_core, me_c), device_id_type=MESH,
-                        )
-                    )
-
+
+    def wait_bytes(buf, count, sem):
+        some = buf.at[pl.ds(0, count)]
+        pltpu.make_async_copy(some, some, sem).wait()
+
+    def finish_sum(ga, gb, stage):
         @pl.when(core == 1)
         def _():
-            for n in range(2 * ncol):
-                if n != ncol:
-                    arrival(ga, 0, ar_sem.at[stage, n]).wait_recv()
+            wait_bytes(ga, 2 * ncol - 1, ar_sem.at[stage])
             if stage == 0:
                 pl.semaphore_wait(near_sem.at[1], len(second_ring))
             gb[z] = add_up(ga, 2 * ncol)
-            for copy in again:
-                copy.start()
-
-        if stage == 0:
-            pl.when(core == 0)(lambda: pl.semaphore_wait(near_sem.at[1], len(second_ring)))
-        for d, copy in out:
-            if d == 0:
-                pl.when(core == 0)(copy.wait_send)
-            else:
-                copy.wait_send()
-        for dz in range(nz):
-            come = arrival(gb, 0, ar_sem.at[stage + 1, dz])
-            if dz == 0:
-                pl.when(core == 0)(come.wait_recv)
-            else:
-                come.wait_recv()
-        return add_up(gb, nz), again
-
-    def settle(again):
+            for dz in sorted(range(nz), key=lambda d: -min(d, nz - d)):
+                for to_core in (0, 1):
+                    if dz or to_core == 0:
+                        pltpu.make_async_remote_copy(
+                            src_ref=gb.at[z], dst_ref=gb.at[z],
+                            send_sem=as_sem.at[stage + 1], recv_sem=ar_sem.at[stage + 1],
+                            device_id=(2 * lax.rem(z + dz, nz) + to_core, me_c), device_id_type=MESH,
+                        ).start()
+            wait_bytes(ga, ncol - 1, as_sem.at[stage])
+            wait_bytes(gb, nz - 1, ar_sem.at[stage + 1])
+
+        @pl.when(core == 0)
+        def _():
+            if stage == 0:
+                pl.semaphore_wait(near_sem.at[1], len(second_ring))
+            wait_bytes(ga, ncol, as_sem.at[stage])
+            wait_bytes(gb, nz, ar_sem.at[stage + 1])
+
+        return add_up(gb, nz)
+
+    def settle(stage):
         @pl.when(core == 1)
         def _():
-            for copy in again:
-                copy.wait_send()
+            wait_bytes(ga, 2 * nz - 1, as_sem.at[stage])
 
     def gather(accs):
         packed = jnp.zeros((8, LANE), jnp.float32)
@@ -528,7 +511,7 @@
     def spread(row, k):
         return jnp.broadcast_to(row[:, k : k + 1], (1, LANE))
 
-    out1 = start_sum(gather((nu0, nu1, nu2, nu3, nu4, nu5, s_q, s_qb, s_q1, s_q2)), ga, gb, 0)
+    start_sum(gather((nu0, nu1, nu2, nu3, nu4, nu5, s_q, s_qb, s_q1, s_q2)), ga, gb, 0)
 
     for copy, _, here in sends[10:]:
         when(*here)(copy.wait_recv)
@@ -555,7 +538,7 @@
 
     for copy, there, _ in sends:
         when(*there)(copy.wait_send)
-    sums, again1 = finish_sum(out1, ga, gb, 0)
+    sums = finish_sum(ga, gb, 0)
 
     c0, c1, c2 = solve([spread(sums, k) for k in range(6)])
     t_q, t_qb, t_q1, t_q2 = [spread(sums, k) for k in range(6, 10)]
@@ -598,7 +581,7 @@
         put(U2, r, n, u2)
         return None if accs is None else add(accs, ((u1, u2), (u2, u2)))
 
-    mu3, mu4 = over_rows(pass4, blank(2))
+    mu3, mu4 = over_rows(pass4, blank(2), False)
 
     def pass5(i, acc):
         return fold(acc, face_terms(U2, pl.multiple_of(TOP + i * step_rows, TOP), step_rows, ext))
@@ -606,10 +589,10 @@
     mu5 = lax.fori_loop(0, rows // step_rows, pass5, zero)
 
 
-    out2 = start_sum(gather((mu0, mu1, mu2, mu3, mu4, mu5)), gc, gd, 2)
+    start_sum(gather((mu0, mu1, mu2, mu3, mu4, mu5)), gc, gd, 2)
     erg_ref[...] = (t_qb - DISCOUNT * (c0 * t_qb + (c1 * t_q1 + c2 * t_q2))) / t_q
-    settle(again1)
-    sums, again2 = finish_sum(out2, gc, gd, 2)
+    settle(1)
+    sums = finish_sum(gc, gd, 2)
     d0, d1, d2 = solve([spread(sums, k) for k in range(6)])
 
     def last_pass(i, carry):
@@ -620,7 +603,7 @@
         return carry
 
     lax.fori_loop(0, rows // step_rows, last_pass, 0)
-    settle(again2)
+    settle(3)
 
 
 def store_kernel(val_ref, den_ref, val_hbm, den_hbm, sem):
@@ -641,9 +624,8 @@
         pile = rows // 8
         big = pltpu.VMEM((ext, rows + 2 * TOP, LANE), jnp.float32)
         plain = pltpu.VMEM((tiles, rows, LANE), jnp.float32)
-        most = max(nrow, ncol)
         value, density, ergodic = pl.pallas_call(
-            functools.partial(kernel, nrow, ncol, 4 if ncol % 4 == 0 else 1, rows, tiles, min(rows, 64)),
+            functools.partial(kernel, nrow, ncol, 4 if ncol % 4 == 0 else 1, rows, tiles, min(rows, 128)),
             out_shape=(
                 jax.ShapeDtypeStruct((rows, cols), jnp.float32),
                 jax.ShapeDtypeStruct((rows, cols), jnp.float32),
@@ -661,8 +643,8 @@
                 pltpu.SemaphoreType.DMA((4, tiles)),
                 pltpu.SemaphoreType.DMA((12,)),
                 pltpu.SemaphoreType.DMA((12,)),
-                pltpu.SemaphoreType.DMA((4, most)),
-                pltpu.SemaphoreType.DMA((4, 2 * ncol)),
+                pltpu.SemaphoreType.DMA((4,)),
+                pltpu.SemaphoreType.DMA((4,)),
                 pltpu.SemaphoreType.REGULAR((2,)),
             ],
             compiler_params=pltpu.CompilerParams(

time: 37.7 us -> 35.6 us (0.944)
  Pallas kernels: 35.7 us -> 33.7 us
    pallas_call x1, Pallas kernels: 34.7 us -> 32.7 us  [body(): pl.pallas_call(functools.partial(kernel, nrow, ncol, 4 if ncol % 4 == 0 e...]
where the time goes in v4:
time: 35.6 us; the launch traced here: 35.5 us
  Pallas kernels  33.7 us (95%)
  between operations  1.8 us (5%)
    pallas_call x1, Pallas kernels, body(): pl.pallas_call(functools.partial(kernel, nrow, ncol, 4 if ncol % 4 == 0 e...  32.7 us
    pallas_call x1, Pallas kernels, body(): pl.pallas_call(store_kernel, out_shape=(jax.ShapeDtypeStruct((rows, cols)...  0.99 us

profile of v4, /device:TPU:1, one launch (start us, length us, event | category | flops | bytes accessed | tf_op | source)
XLA Modules:
  0.0 35.5 jit_solution(3359682932694878746)
XLA Ops:
  0.6 32.7 %shard_map.67 = (f32[256,512]{1,0:T(8,128)S(1)}, f32[256,512]{1,0:T(8,128)S(1)}, f32[1,128]{1,0:T(1,128)S(1)}) custom-call(f32[256,512]{1,0:T(8,128)} %rc_hbm.1, f32[256,512]{1,0:T(8,128)} %cx_hbm.1, f32[256,512]{1,0:T(8,128)} %cy_hbm.1, f32[256,512]{1,0:T(8,128)} %pr_hbm.1), custom_call_target="tpu_custom_call" | custom-call | tf_op jit(solution)/shard_map/pallas_call | solution.py:627
  33.3 1.0 %shard_map.68 = (f32[256,512]{1,0:T(8,128)}, f32[256,512]{1,0:T(8,128)}) custom-call(f32[256,512]{1,0:T(8,128)S(1)} %get-tuple-element.8.val_ref, f32[256,512]{1,0:T(8,128)S(1)} %get-tuple-element.9.den_ref), custom_call_target="tpu_custom_call" | custom-call | tf_op jit(solution)/shard_map/pallas_call | solution.py:654

commit v5 on v4

--- a/solution.py
+++ b/solution.py
@@ -55,8 +55,11 @@
         return ref.at[:, pl.ds(j * LANE, LANE)]
 
     loads = {}
-    for n, (src, dst, top) in enumerate(((cx_hbm, cx, 0), (cy_hbm, cy, 0), (rc_hbm, rc, 0), (pr_hbm, Q, TOP))):
-        for j in range(tiles):
+    outer_tiles = tuple(sorted({0, tiles - 1}))
+    inner_tiles = tuple(range(1, tiles - 1))
+    fields = ((cx_hbm, cx, 0), (cy_hbm, cy, 0), (rc_hbm, rc, 0), (pr_hbm, Q, TOP))
+    for n, (src, dst, top), js in [(n, f, js) for js in (outer_tiles, inner_tiles) for n, f in enumerate(fields)]:
+        for j in js:
             copy = pltpu.make_async_copy(tile_of(src, j), dst.at[j, pl.ds(top, rows), :], in_sem.at[n, j])
             copy.start()
             loads[n, j] = copy
@@ -131,9 +134,6 @@
     def _():
         no_row(END, sw_at)
 
-    for copy in loads.values():
-        copy.wait()
-
     def fold(acc, v):
         while v.shape[0] > 8:
             n = v.shape[0]
@@ -146,22 +146,29 @@
     def blank(k):
         return tuple(zero for _ in range(k))
 
-    def first(i, accs):
-        r = pl.multiple_of(i * step_rows, step_rows)
-        at = pl.ds(TOP + r, step_rows)
-        terms = [None] * 4
-        for j in range(tiles):
-            a, b = cx[j, pl.ds(r, step_rows), :], cy[j, pl.ds(r, step_rows), :]
-            cost = 0.5 * (a * a + b * b)
-            force = rc[j, pl.ds(r, step_rows), :] + cost
-            C[j, at, :] = (1.0 + cost) * FACE
-            B[j, at, :] = force
-            q = Q[j, at, :]
-            for k, t in enumerate((force * force, q, q * force, q * q)):
-                terms[k] = t if j == 0 else terms[k] + t
-        return tuple(fold(acc, t) for acc, t in zip(accs, terms))
-
-    nu0, s_q, s_qb, mu0 = lax.fori_loop(0, rows // step_rows, first, blank(4))
+    def prepare(js, accs):
+        for n in range(len(fields)):
+            for j in js:
+                loads[n, j].wait()
+
+        def first(i, accs):
+            r = pl.multiple_of(i * step_rows, step_rows)
+            at = pl.ds(TOP + r, step_rows)
+            terms = [None] * 4
+            for j in js:
+                a, b = cx[j, pl.ds(r, step_rows), :], cy[j, pl.ds(r, step_rows), :]
+                cost = 0.5 * (a * a + b * b)
+                force = rc[j, pl.ds(r, step_rows), :] + cost
+                C[j, at, :] = (1.0 + cost) * FACE
+                B[j, at, :] = force
+                q = Q[j, at, :]
+                for k, t in enumerate((force * force, q, q * force, q * q)):
+                    terms[k] = t if terms[k] is None else terms[k] + t
+            return tuple(fold(acc, t) for acc, t in zip(accs, terms))
+
+        return lax.fori_loop(0, rows // step_rows, first, accs)
+
+    sums0 = prepare(outer_tiles, blank(4))
 
     parts = LANE // 16
     pile = rows // parts
@@ -206,6 +213,10 @@
     send(pack_w.at[low, :], from_e.at[sw_at, :], (up, west), (not_first, not_west), (not_last, not_east))
     send(pack_e, from_w.at[pl.ds(0, pile), :], (me_r, east), (not_east,), (not_west,))
     send(pack_w, from_e.at[pl.ds(0, pile), :], (me_r, west), (not_west,), (not_east,))
+    if inner_tiles:
+        sums0 = prepare(inner_tiles, sums0)
+    nu0, s_q, s_qb, mu0 = sums0
+
     body = pl.ds(0, tiles)
     for f in (C, B, Q):
         send(f.at[body, pl.ds(TOP, HALO), :], f.at[body, pl.ds(END, HALO), :], (up, me_c), (not_first,), (not_last,))
@@ -271,7 +282,7 @@
             keep,
         )
 
-    def over_rows(step, accs, above=True):
+    def over_rows(step, accs, above=True, unrolled=False):
         if above:
             step(TOP - HALO, HALO, None, has_n)
         step(END, HALO, None, has_s)
@@ -279,6 +290,10 @@
         def loop(i, accs):
             return step(pl.multiple_of(TOP + i * step_rows, TOP), step_rows, accs, None)
 
+        if unrolled:
+            for i in range(rows // step_rows):
+                accs = step(TOP + i * step_rows, step_rows, accs, None)
+            return accs
         return lax.fori_loop(0, rows // step_rows, loop, accs)
 
     def weights_and_v1(r, n, count, keep):
@@ -573,7 +588,7 @@
             return None
         return add(accs, ((q, u1), (u1, u1)))
 
-    mu1, mu2 = over_rows(pass3, blank(2))
+    mu1, mu2 = over_rows(pass3, blank(2), unrolled=True)
 
     def pass4(r, n, accs, keep):
         u1 = rows_of(U1, r, n)
@@ -581,12 +596,11 @@
         put(U2, r, n, u2)
         return None if accs is None else add(accs, ((u1, u2), (u2, u2)))
 
-    mu3, mu4 = over_rows(pass4, blank(2), False)
-
-    def pass5(i, acc):
-        return fold(acc, face_terms(U2, pl.multiple_of(TOP + i * step_rows, TOP), step_rows, ext))
-
-    mu5 = lax.fori_loop(0, rows // step_rows, pass5, zero)
+    mu3, mu4 = over_rows(pass4, blank(2), False, True)
+
+    mu5 = zero
+    for i in range(rows // step_rows):
+        mu5 = fold(mu5, face_terms(U2, TOP + i * step_rows, step_rows, ext))
 
 
     start_sum(gather((mu0, mu1, mu2, mu3, mu4, mu5)), gc, gd, 2)

time: 35.6 us -> 35.1 us (0.986)
  Pallas kernels: 33.7 us -> 33.1 us
    pallas_call x1, Pallas kernels: 32.7 us -> 32.2 us  [body(): pl.pallas_call(functools.partial(kernel, nrow, ncol, 4 if ncol % 4 == 0 e...]
where the time goes in v5:
time: 35.1 us; the launch traced here: 34.9 us
  Pallas kernels  33.1 us (94%)
  between operations  1.8 us (5%)
    pallas_call x1, Pallas kernels, body(): pl.pallas_call(functools.partial(kernel, nrow, ncol, 4 if ncol % 4 == 0 e...  32.2 us
    pallas_call x1, Pallas kernels, body(): pl.pallas_call(store_kernel, out_shape=(jax.ShapeDtypeStruct((rows, cols)...  0.99 us

profile of v5, /device:TPU:1, one launch (start us, length us, event | category | flops | bytes accessed | tf_op | source)
XLA Modules:
  0.0 34.9 jit_solution(16585573998955561250)
XLA Ops:
  0.6 32.2 %shard_map.67 = (f32[256,512]{1,0:T(8,128)S(1)}, f32[256,512]{1,0:T(8,128)S(1)}, f32[1,128]{1,0:T(1,128)S(1)}) custom-call(f32[256,512]{1,0:T(8,128)} %rc_hbm.1, f32[256,512]{1,0:T(8,128)} %cx_hbm.1, f32[256,512]{1,0:T(8,128)} %cy_hbm.1, f32[256,512]{1,0:T(8,128)} %pr_hbm.1), custom_call_target="tpu_custom_call" | custom-call | tf_op jit(solution)/shard_map/pallas_call | solution.py:641
  32.8 1.0 %shard_map.68 = (f32[256,512]{1,0:T(8,128)}, f32[256,512]{1,0:T(8,128)}) custom-call(f32[256,512]{1,0:T(8,128)S(1)} %get-tuple-element.8.val_ref, f32[256,512]{1,0:T(8,128)S(1)} %get-tuple-element.9.den_ref), custom_call_target="tpu_custom_call" | custom-call | tf_op jit(solution)/shard_map/pallas_call | solution.py:668

commit v6 on v5

--- a/solution.py
+++ b/solution.py
@@ -517,6 +517,48 @@
         def _():
             wait_bytes(ga, 2 * nz - 1, as_sem.at[stage])
 
+    chips = nz * ncol
+
+    def start_direct(part):
+        slot = me_r * ncol + me_c
+        gc[slot] = part
+        zs = [2 * lax.rem(z + d, nz) + 1 for d in range(nz)]
+        cs = [[ny * lax.rem(x + a, nx) + lax.rem(y + b, ny) for b in range(ny)] for a in range(nx)]
+
+        def hops(o):
+            return min(o[0], nz - o[0]) + min(o[1], nx - o[1]) + min(o[2], ny - o[2])
+
+        every = [(d, a, b) for d in range(nz) for a in range(nx) for b in range(ny)]
+        for o in sorted(every, key=lambda o: -hops(o)):
+            copy = pltpu.make_async_remote_copy(
+                src_ref=gc.at[slot], dst_ref=gc.at[slot], send_sem=as_sem.at[2], recv_sem=ar_sem.at[2],
+                device_id=(zs[o[0]], cs[o[1]][o[2]]), device_id_type=MESH,
+            )
+            if hops(o) == 0:
+                pl.when(core == 0)(copy.start)
+            else:
+                copy.start()
+
+    hand_over = pltpu.make_async_remote_copy(
+        src_ref=gd.at[0], dst_ref=gd.at[0], send_sem=as_sem.at[3], recv_sem=ar_sem.at[3],
+        device_id=(2 * z, me_c), device_id_type=MESH,
+    )
+
+    def finish_direct():
+        @pl.when(core == 1)
+        def _():
+            wait_bytes(gc, 2 * chips - 1, ar_sem.at[2])
+            gd[0] = jnp.sum(gc[...], axis=0)
+            hand_over.start()
+            wait_bytes(gc, chips - 1, as_sem.at[2])
+
+        @pl.when(core == 0)
+        def _():
+            wait_bytes(gc, chips, as_sem.at[2])
+            wait_bytes(gd, 1, ar_sem.at[3])
+
+        return gd[0]
+
     def gather(accs):
         packed = jnp.zeros((8, LANE), jnp.float32)
         for k, acc in enumerate(accs):
@@ -603,10 +645,10 @@
         mu5 = fold(mu5, face_terms(U2, TOP + i * step_rows, step_rows, ext))
 
 
-    start_sum(gather((mu0, mu1, mu2, mu3, mu4, mu5)), gc, gd, 2)
+    start_direct(gather((mu0, mu1, mu2, mu3, mu4, mu5)))
     erg_ref[...] = (t_qb - DISCOUNT * (c0 * t_qb + (c1 * t_q1 + c2 * t_q2))) / t_q
     settle(1)
-    sums = finish_sum(gc, gd, 2)
+    sums = finish_direct()
     d0, d1, d2 = solve([spread(sums, k) for k in range(6)])
 
     def last_pass(i, carry):
@@ -617,7 +659,7 @@
         return carry
 
     lax.fori_loop(0, rows // step_rows, last_pass, 0)
-    settle(3)
+    pl.when(core == 1)(hand_over.wait_send)
 
 
 def store_kernel(val_ref, den_ref, val_hbm, den_hbm, sem):
@@ -652,7 +694,8 @@
             + [pltpu.VMEM((pile, LANE), jnp.float32)] * 2
             + [pltpu.VMEM((pile + 16, LANE), jnp.float32)] * 2
             + [pltpu.VMEM((2, pile + 16, LANE), jnp.float32)] * 4
-            + [pltpu.VMEM((2 * ncol, 1, LANE), jnp.float32), pltpu.VMEM((nrow // 2, 1, LANE), jnp.float32)] * 2
+            + [pltpu.VMEM((2 * ncol, 1, LANE), jnp.float32), pltpu.VMEM((nrow // 2, 1, LANE), jnp.float32)]
+            + [pltpu.VMEM((nrow * ncol, 1, LANE), jnp.float32), pltpu.VMEM((1, 1, LANE), jnp.float32)]
             + [
                 pltpu.SemaphoreType.DMA((4, tiles)),
                 pltpu.SemaphoreType.DMA((12,)),

time: 35.1 us -> 34.7 us (0.989)
    pallas_call x1, Pallas kernels: 32.2 us -> 31.8 us  [body(): pl.pallas_call(functools.partial(kernel, nrow, ncol, 4 if ncol % 4 == 0 e...]
where the time goes in v6:
time: 34.7 us; the launch traced here: 34.6 us
  Pallas kernels  32.8 us (95%)
  between operations  1.8 us (5%)
    pallas_call x1, Pallas kernels, body(): pl.pallas_call(functools.partial(kernel, nrow, ncol, 4 if ncol % 4 == 0 e...  31.8 us
    pallas_call x1, Pallas kernels, body(): pl.pallas_call(store_kernel, out_shape=(jax.ShapeDtypeStruct((rows, cols)...  0.99 us

profile of v6, /device:TPU:1, one launch (start us, length us, event | category | flops | bytes accessed | tf_op | source)
XLA Modules:
  0.0 34.6 jit_solution(9607093595549724386)
XLA Ops:
  0.6 31.8 %shard_map.67 = (f32[256,512]{1,0:T(8,128)S(1)}, f32[256,512]{1,0:T(8,128)S(1)}, f32[1,128]{1,0:T(1,128)S(1)}) custom-call(f32[256,512]{1,0:T(8,128)} %rc_hbm.1, f32[256,512]{1,0:T(8,128)} %cx_hbm.1, f32[256,512]{1,0:T(8,128)} %cy_hbm.1, f32[256,512]{1,0:T(8,128)} %pr_hbm.1), custom_call_target="tpu_custom_call" | custom-call | tf_op jit(solution)/shard_map/pallas_call | solution.py:683
  32.4 1.0 %shard_map.68 = (f32[256,512]{1,0:T(8,128)}, f32[256,512]{1,0:T(8,128)}) custom-call(f32[256,512]{1,0:T(8,128)S(1)} %get-tuple-element.8.val_ref, f32[256,512]{1,0:T(8,128)S(1)} %get-tuple-element.9.den_ref), custom_call_target="tpu_custom_call" | custom-call | tf_op jit(solution)/shard_map/pallas_call | solution.py:711

commit v7 on v5

--- a/solution.py
+++ b/solution.py
@@ -41,7 +41,7 @@
     rc_hbm, cx_hbm, cy_hbm, pr_hbm,
     val_ref, den_ref, erg_ref,
     cx, cy, rc, C, B, Q, WE, WW, WS, CE, V1, V2, X, LP, U1, U2,
-    pack_e, pack_w, from_w, from_e, SC, SB, S1, S2, ga, gb, gc, gd,
+    pack_e, pack_w, from_w, from_e, SC, SB, S1, S2, ga, gb, gc,
     in_sem, hs_sem, hr_sem, as_sem, ar_sem, near_sem,
 ):
     me_r = lax.axis_index("row")
@@ -349,10 +349,9 @@
         step(TOP + 8, 8, None)
         step(END - 16, 8, None)
 
-        def loop(i, accs):
-            return step(pl.multiple_of(TOP + INNER + i * part, 8), part, accs)
-
-        return lax.fori_loop(0, pieces, loop, accs)
+        for i in range(pieces):
+            accs = step(TOP + INNER + i * part, part, accs)
+        return accs
 
     def center1(r, n, accs):
         v1 = weights_and_v1(r, n, tiles, None)
@@ -366,12 +365,11 @@
             return None
         return add(accs, ((v1, v2), (v2, v2), (rows_of(Q, r, n, tiles), v2)), weigh)
 
-    def center3(i, acc):
-        return fold(acc, face_terms(V2, pl.multiple_of(TOP + INNER + i * part, 8), part, tiles, weigh))
-
     nu1, nu2, s_q1 = over_center(center1, blank(3))
     nu3, nu4, s_q2 = over_center(center2, blank(3))
-    nu5 = lax.fori_loop(0, pieces, center3, zero)
+    nu5 = zero
+    for i in range(pieces):
+        nu5 = fold(nu5, face_terms(V2, TOP + INNER + i * part, part, tiles, weigh))
 
     def own_columns(f, j, shift):
         acc = jnp.zeros((pile, LANE), jnp.float32)
@@ -517,6 +515,33 @@
         def _():
             wait_bytes(ga, 2 * nz - 1, as_sem.at[stage])
 
+    others = nrow * ncol - 1
+
+    def start_direct(part):
+        slot = me_r * ncol + me_c
+        gc[slot] = part
+        zs = [2 * lax.rem(z + d, nz) for d in range(nz)]
+        cs = [[ny * lax.rem(x + a, nx) + lax.rem(y + b, ny) for b in range(ny)] for a in range(nx)]
+
+        def hops(o):
+            return min(o[0], nz - o[0]) + min(o[1], nx - o[1]) + min(o[2], ny - o[2])
+
+        every = [(d, a, b) for d in range(nz) for a in range(nx) for b in range(ny)]
+        for to_core in (1, 0):
+            for o in sorted(every, key=lambda o: -hops(o)):
+                copy = pltpu.make_async_remote_copy(
+                    src_ref=gc.at[slot], dst_ref=gc.at[slot], send_sem=as_sem.at[2], recv_sem=ar_sem.at[2],
+                    device_id=(zs[o[0]] + to_core, cs[o[1]][o[2]]), device_id_type=MESH,
+                )
+                if hops(o) == 0:
+                    pl.when(core == 1 - to_core)(copy.start)
+                else:
+                    copy.start()
+
+    def finish_direct():
+        wait_bytes(gc, others, ar_sem.at[2])
+        return jnp.sum(gc[...], axis=0)
+
     def gather(accs):
         packed = jnp.zeros((8, LANE), jnp.float32)
         for k, acc in enumerate(accs):
@@ -564,10 +589,10 @@
         put(X, r, n, value)
         if keep is None:
             for j in range(tiles):
-                val_ref[pl.ds(pl.multiple_of(r - TOP, 8), n), pl.ds(j * LANE, LANE)] = value[j]
+                val_ref[pl.ds(r - TOP, n), pl.ds(j * LANE, LANE)] = value[j]
         return accs
 
-    over_rows(pass_x, 0)
+    over_rows(pass_x, 0, unrolled=True)
 
     def pass3(r, n, accs, keep):
         last, start = masks(n)
@@ -603,10 +628,10 @@
         mu5 = fold(mu5, face_terms(U2, TOP + i * step_rows, step_rows, ext))
 
 
-    start_sum(gather((mu0, mu1, mu2, mu3, mu4, mu5)), gc, gd, 2)
+    start_direct(gather((mu0, mu1, mu2, mu3, mu4, mu5)))
     erg_ref[...] = (t_qb - DISCOUNT * (c0 * t_qb + (c1 * t_q1 + c2 * t_q2))) / t_q
     settle(1)
-    sums = finish_sum(gc, gd, 2)
+    sums = finish_direct()
     d0, d1, d2 = solve([spread(sums, k) for k in range(6)])
 
     def last_pass(i, carry):
@@ -617,7 +642,7 @@
         return carry
 
     lax.fori_loop(0, rows // step_rows, last_pass, 0)
-    settle(3)
+    wait_bytes(gc, others, as_sem.at[2])
 
 
 def store_kernel(val_ref, den_ref, val_hbm, den_hbm, sem):
@@ -652,7 +677,8 @@
             + [pltpu.VMEM((pile, LANE), jnp.float32)] * 2
             + [pltpu.VMEM((pile + 16, LANE), jnp.float32)] * 2
             + [pltpu.VMEM((2, pile + 16, LANE), jnp.float32)] * 4
-            + [pltpu.VMEM((2 * ncol, 1, LANE), jnp.float32), pltpu.VMEM((nrow // 2, 1, LANE), jnp.float32)] * 2
+            + [pltpu.VMEM((2 * ncol, 1, LANE), jnp.float32), pltpu.VMEM((nrow // 2, 1, LANE), jnp.float32)]
+            + [pltpu.VMEM((nrow * ncol, 1, LANE), jnp.float32)]
             + [
                 pltpu.SemaphoreType.DMA((4, tiles)),
                 pltpu.SemaphoreType.DMA((12,)),

time: 35.1 us -> 34.3 us (0.977)
  Pallas kernels: 33.1 us -> 32.3 us
    pallas_call x1, Pallas kernels: 32.2 us -> 31.3 us  [body(): pl.pallas_call(functools.partial(kernel, nrow, ncol, 4 if ncol % 4 == 0 e...]
where the time goes in v7:
time: 34.3 us; the launch traced here: 34.1 us
  Pallas kernels  32.3 us (94%)
  between operations  1.8 us (5%)
    pallas_call x1, Pallas kernels, body(): pl.pallas_call(functools.partial(kernel, nrow, ncol, 4 if ncol % 4 == 0 e...  31.3 us
    pallas_call x1, Pallas kernels, body(): pl.pallas_call(store_kernel, out_shape=(jax.ShapeDtypeStruct((rows, cols)...  0.99 us

profile of v7, /device:TPU:1, one launch (start us, length us, event | category | flops | bytes accessed | tf_op | source)
XLA Modules:
  0.0 34.1 jit_solution(233000527597909936)
XLA Ops:
  0.6 31.3 %shard_map.67 = (f32[256,512]{1,0:T(8,128)S(1)}, f32[256,512]{1,0:T(8,128)S(1)}, f32[1,128]{1,0:T(1,128)S(1)}) custom-call(f32[256,512]{1,0:T(8,128)} %rc_hbm.1, f32[256,512]{1,0:T(8,128)} %cx_hbm.1, f32[256,512]{1,0:T(8,128)} %cy_hbm.1, f32[256,512]{1,0:T(8,128)} %pr_hbm.1), custom_call_target="tpu_custom_call" | custom-call | tf_op jit(solution)/shard_map/pallas_call | solution.py:666
  32.0 1.0 %shard_map.68 = (f32[256,512]{1,0:T(8,128)}, f32[256,512]{1,0:T(8,128)}) custom-call(f32[256,512]{1,0:T(8,128)S(1)} %get-tuple-element.8.val_ref, f32[256,512]{1,0:T(8,128)S(1)} %get-tuple-element.9.den_ref), custom_call_target="tpu_custom_call" | custom-call | tf_op jit(solution)/shard_map/pallas_call | solution.py:694

commit v8 on v7

--- a/solution.py
+++ b/solution.py
@@ -152,7 +152,7 @@
                 loads[n, j].wait()
 
         def first(i, accs):
-            r = pl.multiple_of(i * step_rows, step_rows)
+            r = i * step_rows
             at = pl.ds(TOP + r, step_rows)
             terms = [None] * 4
             for j in js:
@@ -166,7 +166,9 @@
                     terms[k] = t if terms[k] is None else terms[k] + t
             return tuple(fold(acc, t) for acc, t in zip(accs, terms))
 
-        return lax.fori_loop(0, rows // step_rows, first, accs)
+        for i in range(rows // step_rows):
+            accs = first(i, accs)
+        return accs
 
     sums0 = prepare(outer_tiles, blank(4))
 
@@ -635,13 +637,14 @@
     d0, d1, d2 = solve([spread(sums, k) for k in range(6)])
 
     def last_pass(i, carry):
-        r = pl.multiple_of(i * step_rows, step_rows)
+        r = i * step_rows
         at = pl.ds(TOP + r, step_rows)
         for j in range(tiles):
             den_ref[pl.ds(r, step_rows), pl.ds(j * LANE, LANE)] = d0 * Q[j, at, :] + (d1 * U1[j, at, :] + d2 * U2[j, at, :])
         return carry
 
-    lax.fori_loop(0, rows // step_rows, last_pass, 0)
+    for i in range(rows // step_rows):
+        last_pass(i, 0)
     wait_bytes(gc, others, as_sem.at[2])
 
 

time: 34.3 us -> 34.3 us (level)
  no operation moved by 1% of the time
where the time goes in v8:
time: 34.3 us; the launch traced here: 34.2 us
  Pallas kernels  32.3 us (94%)
  between operations  1.8 us (5%)
    pallas_call x1, Pallas kernels, body(): pl.pallas_call(functools.partial(kernel, nrow, ncol, 4 if ncol % 4 == 0 e...  31.4 us
    pallas_call x1, Pallas kernels, body(): pl.pallas_call(store_kernel, out_shape=(jax.ShapeDtypeStruct((rows, cols)...  0.99 us

profile of v8, /device:TPU:1, one launch (start us, length us, event | category | flops | bytes accessed | tf_op | source)
XLA Modules:
  0.0 34.2 jit_solution(5902813359184638900)
XLA Ops:
  0.6 31.4 %shard_map.67 = (f32[256,512]{1,0:T(8,128)S(1)}, f32[256,512]{1,0:T(8,128)S(1)}, f32[1,128]{1,0:T(1,128)S(1)}) custom-call(f32[256,512]{1,0:T(8,128)} %rc_hbm.1, f32[256,512]{1,0:T(8,128)} %cx_hbm.1, f32[256,512]{1,0:T(8,128)} %cy_hbm.1, f32[256,512]{1,0:T(8,128)} %pr_hbm.1), custom_call_target="tpu_custom_call" | custom-call | tf_op jit(solution)/shard_map/pallas_call | solution.py:669
  32.0 1.0 %shard_map.68 = (f32[256,512]{1,0:T(8,128)}, f32[256,512]{1,0:T(8,128)}) custom-call(f32[256,512]{1,0:T(8,128)S(1)} %get-tuple-element.8.val_ref, f32[256,512]{1,0:T(8,128)S(1)} %get-tuple-element.9.den_ref), custom_call_target="tpu_custom_call" | custom-call | tf_op jit(solution)/shard_map/pallas_call | solution.py:697
